TPU v7x, 128 devices: a whole 4x4x4 slice. The times are simulated.
128 devices in a mesh: batch: 1, graph: 128 (over z, y, x, core).
Axes of the slice: x: 4, y: 4, z: 4, core: 2. Of those that a mesh axis runs over, the one named last changes fastest.
Arguments:
- grid_feat: float32 [65536, 102], P(('batch', 'graph'))
- mesh_feat: float32 [65536, 3], P(('batch', 'graph'))
- edge_feat: float32 [1048576, 4], P(('batch', 'graph'))
- need_rows: int32 [1048576], P(('batch', 'graph'))
- edge_src: int32 [1048576], P(('batch', 'graph'))
- edge_dst: int32 [1048576], P(('batch', 'graph'))
- edge_mask: int32 [1048576], P(('batch', 'graph'))
- w_grid_emb: bfloat16 [102, 1024], replicated
- w_mesh_emb: bfloat16 [3, 1024], replicated
- w_edge_emb: bfloat16 [4, 1024], replicated
- w_edge_upd: bfloat16 [3072, 1024], replicated
- w_mesh_upd: bfloat16 [2048, 1024], replicated
- w_grid_upd: bfloat16 [1024, 1024], replicated
- w_second: bfloat16 [6, 1024, 1024], replicated
- mlp_vecs: bfloat16 [6, 4, 1024], replicated
Outputs:
- output 1: bfloat16 [65536, 1024], P(('batch', 'graph'))
- output 2: bfloat16 [65536, 1024], P(('batch', 'graph'))
All inputs are finite; a program needn't handle non-finite values.
Results may differ from a plain program's by a relative error of at most 0.00922038.
Values are sent between devices in bfloat16 or wider.
A program may use at most 1 GiB of HBM per device.

v0:
```python
import jax
import jax.numpy as jnp
from jax import lax
from jax.sharding import PartitionSpec as P

LN_EPS = 1e-5


def mlp_tail(pre_act, w_out, params):
    hidden = jax.nn.silu(pre_act + params[0].astype(jnp.float32)).astype(jnp.bfloat16)
    result = jnp.dot(hidden, w_out, preferred_element_type=jnp.float32) + params[1].astype(jnp.float32)
    mean = jnp.mean(result, axis=-1, keepdims=True)
    centered = result - mean
    variance = jnp.mean(centered * centered, axis=-1, keepdims=True)
    return centered * lax.rsqrt(variance + LN_EPS) * params[2].astype(jnp.float32) + params[3].astype(jnp.float32)


def embed(features, w_in, w_out, params):
    pre_act = jnp.dot(features.astype(jnp.bfloat16), w_in, preferred_element_type=jnp.float32)
    return mlp_tail(pre_act, w_out, params).astype(jnp.bfloat16)


def residual(base, pre_act, w_out, params):
    return (base.astype(jnp.float32) + mlp_tail(pre_act, w_out, params)).astype(jnp.bfloat16)


def grid_step(grid_feat, w_grid_emb, w_grid_upd, w_second, mlp_vecs):
    grid_emb = embed(grid_feat, w_grid_emb, w_second[0], mlp_vecs[0])
    pre_act = jnp.dot(grid_emb, w_grid_upd, preferred_element_type=jnp.float32)
    return grid_emb, residual(grid_emb, pre_act, w_second[5], mlp_vecs[5])


def mesh_step(table, mesh_feat, edge_feat, edge_src, edge_dst, edge_mask,
              w_mesh_emb, w_edge_emb, w_edge_upd, w_mesh_upd, w_second, mlp_vecs):
    width = w_second.shape[-1]
    mesh_nodes = mesh_feat.shape[0]
    mesh_emb = embed(mesh_feat, w_mesh_emb, w_second[1], mlp_vecs[1])
    edge_emb = embed(edge_feat, w_edge_emb, w_second[2], mlp_vecs[2])
    table_proj = jnp.dot(table, w_edge_upd[width:2 * width], preferred_element_type=jnp.float32)
    mesh_proj = jnp.dot(mesh_emb, w_edge_upd[2 * width:], preferred_element_type=jnp.float32)
    pre_edge = (jnp.dot(edge_emb, w_edge_upd[:width], preferred_element_type=jnp.float32)
                + jnp.take(table_proj, edge_src, axis=0) + jnp.take(mesh_proj, edge_dst, axis=0))
    edge_new = residual(edge_emb, pre_edge, w_second[3], mlp_vecs[3])
    node_ids = jnp.arange(mesh_nodes, dtype=jnp.int32)
    incidence = ((edge_dst[:, None] == node_ids[None, :]) & (edge_mask[:, None] > 0)).astype(jnp.bfloat16)
    aggregated = jnp.einsum('em,ed->md', incidence, edge_new, preferred_element_type=jnp.float32).astype(jnp.bfloat16)
    pre_mesh = (jnp.dot(mesh_emb, w_mesh_upd[:width], preferred_element_type=jnp.float32)
                + jnp.dot(aggregated, w_mesh_upd[width:], preferred_element_type=jnp.float32))
    return residual(mesh_emb, pre_mesh, w_second[4], mlp_vecs[4])


def solution(mesh):
    ngraph = mesh.shape['graph']
    sharded = P(('batch', 'graph'))
    replicated = P()

    def local_step(grid_feat, mesh_feat, edge_feat, need_rows, edge_src, edge_dst, edge_mask,
                   w_grid_emb, w_mesh_emb, w_edge_emb, w_edge_upd, w_mesh_upd, w_grid_upd, w_second, mlp_vecs):
        width = w_second.shape[-1]
        slots = need_rows.shape[0] // ngraph
        requests = lax.all_to_all(need_rows.reshape(ngraph, slots), 'graph', 0, 0, tiled=True)
        grid_emb, grid_out = grid_step(grid_feat, w_grid_emb, w_grid_upd, w_second, mlp_vecs)
        outgoing = jnp.take(grid_emb, requests, axis=0)
        table = lax.all_to_all(outgoing, 'graph', 0, 0, tiled=True).reshape(ngraph * slots, width)
        mesh_out = mesh_step(table, mesh_feat, edge_feat, edge_src, edge_dst, edge_mask,
                             w_mesh_emb, w_edge_emb, w_edge_upd, w_mesh_upd, w_second, mlp_vecs)
        return mesh_out, grid_out

    return jax.shard_map(local_step, mesh=mesh,
                         in_specs=(sharded,) * 7 + (replicated,) * 8,
                         out_specs=(sharded, sharded), check_vma=False)
```

profile of v0, /device:TPU:37, one launch (start us, length us, event | category | flops | bytes accessed | tf_op | source)
XLA Modules:
  0.0 549.6 jit_solution(5552086916478665394)
XLA Ops:
  0.6 0.0 copy-start
  0.6 1.6 all_to_all.13
  2.3 10.5 %all-to-all-start = ((s32[128,1,64]{2,1,0:T(1,128)}), s32[128,1,64]{2,1,0:T(1,128)S(1)}, u32[]{:S(2)}, u32[]{:S(2)}) async-start(s32[128,1,64]{2,1,0:T(1,128)} %bitcast.10), calls=%async_computation | async-start | bytes 131072 | tf_op jit(solution)/shard_map/all_to_all | solution.py:61
  12.8 1.6 slice_convert_fusion.2
  14.4 4.8 add_reduce_fusion.4
  19.2 2.1 multiply_reduce_fusion.4
  21.4 0.0 copy-done.12
  21.4 0.0 copy-done.19
  21.4 0.0 copy-done.21
  21.4 0.0 copy-done.2
  21.4 0.4 add_convert_fusion.5
  21.9 0.0 copy-done.23
  21.9 0.1 copy-done.26
  22.0 1.4 slice_convert_fusion.1
  23.4 0.0 all-to-all-done
  23.5 0.1 reshape.373
  23.5 35.3 %gather_fusion = bf16[8192,1024]{1,0:T(8,128)(2,1)} fusion(bf16[512,1024]{1,0:T(8,128)(2,1)S(1)} %add_convert_fusion.5, s32[8192]{0:T(1024)S(1)} %broadcast_clamp_fusion), kind=kCustom, calls=%fused_computation | custom fusion | bytes 33587200 | tf_op jit(solution)/shard_map/jit(_take)/gather | solution.py:63
  58.9 14.2 %broadcast_select_fusion = bf16[128,64,1024]{2,1,0:T(8,128)(2,1)} fusion(bf16[128,64,1024]{2,1,0:T(8,128)(2,1)} %bitcast.80, pred[128,64]{1,0:T(8,128)(4,1)S(1)} %compare_and_fusion), kind=kLoop, calls=%fused_computation.21 | loop fusion | flops 8388608 | bytes 33562624 | tf_op jit(solution)/shard_map/jit(_take)/select_n | solution.py:63
  73.1 10.7 %all-to-all-start.1 = ((bf16[128,64,1024]{2,1,0:T(8,128)(2,1)}), bf16[128,64,1024]{2,1,0:T(8,128)(2,1)}, u32[]{:S(2)}, u32[]{:S(2)}) async-start(bf16[128,64,1024]{2,1,0:T(8,128)(2,1)} %broadcast_select_fusion), calls=%async_computation.1 | async-start | bytes 33554432 | tf_op jit(solution)/shard_map/all_to_all | solution.py:64
  83.8 0.0 copy-start.9
  83.8 4.6 add_reduce_fusion.5
  88.5 2.1 multiply_reduce_fusion.5
  90.6 0.0 copy-done.33
  90.6 0.0 copy-done.15
  90.7 0.0 copy-done.36
  90.7 0.0 copy-done.4
  90.7 4.3 fusion.30
  94.9 0.0 copy-done.43
  94.9 45.2 %gather_fusion.2 = f32[8192,1024]{1,0:T(8,128)} fusion(f32[512,1024]{1,0:T(8,128)} %fusion.30, s32[8192]{0:T(1024)S(1)} %fusion.55), kind=kCustom, calls=%fused_computation.2 | custom fusion | bytes 67141632 | tf_op jit(solution)/shard_map/jit(_take)/gather | solution.py:42
  140.1 0.0 copy-done.18
  140.1 5.3 add_reduce_fusion.2
  145.4 0.0 copy-start.59
  145.4 2.0 multiply_reduce_fusion.2
  147.5 0.0 copy-done.25
  147.5 0.6 broadcast_compare_fusion
  148.1 0.0 copy-done.8
  148.1 11.7 %multiply_convert_fusion.2.clone.5 = bf16[8192,1024]{1,0:T(8,128)(2,1)} fusion(f32[1024]{0:T(1024)S(1)} %bitcast.127, bf16[4,1024]{1,0:T(4,128)(2,1)S(1)} %copy-done.59, f32[8192,4]{0,1:T(4,128)S(1)} %copy-done.56), kind=kOutput, calls=%fused_computation.8.clone.clone.clone.clone.2 | convolution fusion | flops 117473280 | bytes 16920576 | tf_op jit(solution)/shard_map/dot_general | solution.py:19
  159.9 0.0 copy-done.40
  159.9 26.6 %add_reduce_fusion.1 = (f32[8192]{0:T(1024)S(1)}, f32[8192,1024]{0,1:T(8,128)}) fusion(f32[1024]{0:T(1024)S(1)} %bitcast.113, bf16[6,1024,1024]{2,1,0:T(8,128)(2,1)} %param.28, bf16[8192,1024]{1,0:T(8,128)(2,1)} %multiply_convert_fusion.2.clone.5), kind=kOutput, calls=%fused_computation.10 | convolution fusion | flops 17196638208 | bytes 52465664 | tf_op jit(solution)/shard_map/dot_general | solution.py:11
  186.5 0.0 copy-start.55
  186.5 15.0 %multiply_reduce_fusion.1 = f32[8192]{0:T(1024)S(1)} fusion(f32[8192,1024]{0,1:T(8,128)} %get-tuple-element.31, f32[8192]{0:T(1024)S(1)} %broadcast_multiply_fusion.1, f32[1024]{0:T(1024)S(1)} %bitcast.114), kind=kLoop, calls=%fused_computation.7 | loop fusion | flops 33546240 | bytes 33624064 | tf_op jit(solution)/shard_map/reduce_sum | solution.py:14
  201.6 0.0 copy-done.10
  201.6 0.0 copy-done.3
  201.6 0.0 copy-done.7
  201.6 0.0 copy-done.13
  201.7 0.0 copy-done.20
  201.7 0.0 copy-done.22
  201.7 0.0 copy-done.24
  201.7 0.0 copy-done.27
  201.8 1.9 add_convert_fusion.3
  203.7 2.7 fusion.38
  206.4 124.9 %all-to-all-done.1 = bf16[128,64,1024]{2,1,0:T(8,128)(2,1)} async-done(((bf16[128,64,1024]{2,1,0:T(8,128)(2,1)}), bf16[128,64,1024]{2,1,0:T(8,128)(2,1)}, u32[]{:S(2)}, u32[]{:S(2)}) %all-to-all-start.1) | async-done | bytes 16777248 | tf_op jit(solution)/shard_map/all_to_all | solution.py:64
  331.3 26.1 %fusion.32 = f32[8192,1024]{1,0:T(8,128)} fusion(bf16[8192,1024]{1,0:T(8,128)(2,1)} %bitcast.19, bf16[3072,1024]{1,0:T(8,128)(2,1)} %param.25), kind=kOutput, calls=%fused_computation.49 | convolution fusion | flops 17179869184 | bytes 52428800 | tf_op jit(solution)/shard_map/dot_general | solution.py:39
  357.4 54.1 %gather_fusion.1 = f32[8192,1024]{1,0:T(8,128)} fusion(f32[8192,1024]{1,0:T(8,128)} %fusion.32, s32[8192]{0:T(1024)S(1)} %fusion.54), kind=kCustom, calls=%fused_computation.1 | custom fusion | bytes 67141632 | tf_op jit(solution)/shard_map/jit(_take)/gather | solution.py:42
  411.5 45.9 %multiply_convert_fusion.clone.1.clone.5 = bf16[8192,1024]{1,0:T(8,128)(2,1)} fusion(f32[8192,1024]{1,0:T(8,128)} %gather_fusion.2, f32[8192,1024]{1,0:T(8,128)} %gather_fusion.1, f32[1024]{0:T(1024)S(1)} %bitcast.126, pred[8192]{0:T(1024)(128)(4,1)S(1)} %get-tuple-element.38, pred[8192]{0:T(1024)(128)(4,1)S(1)} %get-tuple-element.39, ...), kind=kOutput, calls=%fused_computation.5.clone.clone.clone.clone.clone.2 | convolution fusion | flops 17314086912 | bytes 119635968 | tf_op jit(solution)/shard_map/dot_general | solution.py:41
  457.4 26.3 %add_reduce_fusion = (f32[8192]{0:T(1024)S(1)}, f32[8192,1024]{0,1:T(8,128)}) fusion(f32[1024]{0:T(1024)S(1)} %bitcast.110, bf16[6,1024,1024]{2,1,0:T(8,128)(2,1)} %param.28, bf16[8192,1024]{1,0:T(8,128)(2,1)} %multiply_convert_fusion.clone.1.clone.5), kind=kOutput, calls=%fused_computation.9 | convolution fusion | flops 17196638208 | bytes 52465664 | tf_op jit(solution)/shard_map/dot_general | solution.py:11
  483.7 0.0 copy-start.46
  483.7 13.4 %multiply_reduce_fusion = f32[8192]{0:T(1024)S(1)} fusion(f32[8192,1024]{0,1:T(8,128)} %get-tuple-element.33, f32[8192]{0:T(1024)S(1)} %broadcast_multiply_fusion, f32[1024]{0:T(1024)S(1)} %bitcast.111), kind=kLoop, calls=%fused_computation.4 | loop fusion | flops 33546240 | bytes 33624064 | tf_op jit(solution)/shard_map/reduce_sum | solution.py:14
  497.3 45.6 %multiply_convert_fusion.4 = bf16[512,1024]{1,0:T(8,128)(2,1)S(1)} fusion(f32[512,1024]{1,0:T(8,128)} %fusion.38, bf16[2048,1024]{1,0:T(8,128)(2,1)} %param.26, f32[8192,1024]{0,1:T(8,128)} %get-tuple-element.33, f32[1024]{0:T(1024)S(1)} %bitcast.120, f32[1024]{0:T(1024)S(1)} %bitcast.121, f32[8192]{0:T(1024)S(1)} %add_rsqrt_fusion, ...), kind=kOutput, calls=%fused_computation.43 | convolution fusion | flops 9797894144 | bytes 72552448 | tf_op jit(solution)/shard_map/dot_general | solution.py:48
  542.9 3.0 add_reduce_fusion.3
  545.9 0.4 multiply_reduce_fusion.3
  546.3 0.0 copy-start.1
  546.3 1.1 copy-done.6
  547.5 1.9 add_convert_fusion.4
  (108 shorter events, 0.4 us)
Async XLA Ops:
  0.6 139.5 %copy-start = (bf16[1024,1024]{1,0:T(8,128)(2,1)S(1)}, bf16[1024,1024]{1,0:T(8,128)(2,1)}, u32[]{:S(2)}) copy-start(bf16[1024,1024]{1,0:T(8,128)(2,1)} %param.27) | copy-start | bytes 6291460
  2.3 21.2 %all-to-all-start = ((s32[128,1,64]{2,1,0:T(1,128)}), s32[128,1,64]{2,1,0:T(1,128)S(1)}, u32[]{:S(2)}, u32[]{:S(2)}) async-start(s32[128,1,64]{2,1,0:T(1,128)} %bitcast.10), calls=%async_computation | async-start | bytes 131072 | tf_op jit(solution)/shard_map/all_to_all | solution.py:61
  14.4 7.0 %copy-start.12 = (f32[1,1,1024]{2,1,0:T(1,128)}, f32[1,1,1024]{2,1,0:T(1,128)S(1)}, u32[]{:S(2)}) copy-start(f32[1,1,1024]{2,1,0:T(1,128)S(1)} %get-tuple-element.14) | copy-start | bytes 12292
  14.4 7.0 %copy-start.19 = (f32[1,1,1024]{2,1,0:T(1,128)}, f32[1,1,1024]{2,1,0:T(1,128)S(1)}, u32[]{:S(2)}) copy-start(f32[1,1,1024]{2,1,0:T(1,128)S(1)} %get-tuple-element.12) | copy-start | bytes 12292
  14.4 7.0 %copy-start.21 = (f32[1,1,1024]{2,1,0:T(1,128)}, f32[1,1,1024]{2,1,0:T(1,128)S(1)}, u32[]{:S(2)}) copy-start(f32[1,1,1024]{2,1,0:T(1,128)S(1)} %get-tuple-element.13) | copy-start | bytes 12292
  14.4 76.2 %copy-start.33 = (f32[1,1,1024]{2,1,0:T(1,128)}, f32[1,1,1024]{2,1,0:T(1,128)S(1)}, u32[]{:S(2)}) copy-start(f32[1,1,1024]{2,1,0:T(1,128)S(1)} %get-tuple-element.20) | copy-start | bytes 12292
  19.2 2.2 copy-start.2
  19.2 2.7 copy-start.23
  21.4 0.6 copy-start.26
  23.4 67.2 %copy-start.15 = (f32[1,1,1024]{2,1,0:T(1,128)}, f32[1,1,1024]{2,1,0:T(1,128)S(1)}, u32[]{:S(2)}) copy-start(f32[1,1,1024]{2,1,0:T(1,128)S(1)} %get-tuple-element.23) | copy-start | bytes 12292
  23.4 67.3 %copy-start.36 = (f32[1,1,1024]{2,1,0:T(1,128)}, f32[1,1,1024]{2,1,0:T(1,128)S(1)}, u32[]{:S(2)}) copy-start(f32[1,1,1024]{2,1,0:T(1,128)S(1)} %get-tuple-element.22) | copy-start | bytes 12292
  73.1 10.7 %copy-start.57 = (bf16[3,1024]{1,0:T(4,128)(2,1)S(1)}, bf16[3,1024]{1,0:T(4,128)(2,1)}, u32[]{:S(2)}) copy-start(bf16[3,1024]{1,0:T(4,128)(2,1)} %param.23) | copy-start | bytes 18436
  73.1 10.7 %copy-start.58 = (f32[512,3]{0,1:T(4,128)S(1)}, f32[512,3]{0,1:T(4,128)}, u32[]{:S(2)}) copy-start(f32[512,3]{0,1:T(4,128)} %param.16) | copy-start | bytes 18436
  73.1 258.2 %all-to-all-start.1 = ((bf16[128,64,1024]{2,1,0:T(8,128)(2,1)}), bf16[128,64,1024]{2,1,0:T(8,128)(2,1)}, u32[]{:S(2)}, u32[]{:S(2)}) async-start(bf16[128,64,1024]{2,1,0:T(8,128)(2,1)} %broadcast_select_fusion), calls=%async_computation.1 | async-start | bytes 33554432 | tf_op jit(solution)/shard_map/all_to_all | solution.py:64
  83.8 6.8 %copy-start.9 = (s32[8192]{0:T(1024)S(1)}, s32[8192]{0:T(1024)}, u32[]{:S(2)}) copy-start(s32[8192]{0:T(1024)} %param.20) | copy-start | bytes 98308
  88.4 2.2 copy-start.4
  88.5 6.5 %copy-start.28 = (f32[512]{0:T(512)}, f32[512]{0:T(512)S(1)}, u32[]{:S(2)}) copy-start(f32[512]{0:T(512)S(1)} %broadcast_multiply_fusion.5) | copy-start | bytes 6148
  90.6 4.3 copy-start.43
  94.9 45.2 %copy-start.18 = (f32[1,1,1024]{2,1,0:T(1,128)S(1)}, f32[1,1,1024]{2,1,0:T(1,128)}, u32[]{:S(2)}) copy-start(f32[1,1,1024]{2,1,0:T(1,128)} %get-tuple-element.2) | copy-start | bytes 12292
  94.9 45.2 %copy-start.54 = (f32[1,1,1024]{2,1,0:T(1,128)S(1)}, f32[1,1,1024]{2,1,0:T(1,128)}, u32[]{:S(2)}) copy-start(f32[1,1,1024]{2,1,0:T(1,128)} %get-tuple-element.3) | copy-start | bytes 12292
  145.4 2.1 copy-start.25
  145.4 2.7 copy-start.8
  145.4 2.7 copy-start.53
  145.4 2.7 copy-start.56
  145.4 2.7 copy-start.59
  148.1 11.7 %copy-start.40 = (f32[1,1,1024]{2,1,0:T(1,128)S(1)}, f32[1,1,1024]{2,1,0:T(1,128)}, u32[]{:S(2)}) copy-start(f32[1,1,1024]{2,1,0:T(1,128)} %get-tuple-element.18) | copy-start | bytes 12292
  186.4 15.1 %copy-start.10 = (s32[8192]{0:T(1024)S(1)}, s32[8192]{0:T(1024)}, u32[]{:S(2)}) copy-start(s32[8192]{0:T(1024)} %param.20) | copy-start | bytes 98308
  186.4 15.2 %copy-start.3 = (f32[512,1024]{1,0:T(8,128)S(1)}, f32[512,1024]{1,0:T(8,128)}, u32[]{:S(2)}) copy-start(f32[512,1024]{1,0:T(8,128)} %get-tuple-element.29) | copy-start | bytes 6291460
  186.5 15.2 %copy-start.7 = (f32[512,1024]{1,0:T(8,128)S(1)}, f32[512,1024]{1,0:T(8,128)}, u32[]{:S(2)}) copy-start(f32[512,1024]{1,0:T(8,128)} %get-tuple-element.37) | copy-start | bytes 6291460
  186.5 15.2 %copy-start.13 = (f32[1,1,1024]{2,1,0:T(1,128)S(1)}, f32[1,1,1024]{2,1,0:T(1,128)}, u32[]{:S(2)}) copy-start(f32[1,1,1024]{2,1,0:T(1,128)} %copy-done.12) | copy-start | bytes 12292
  186.5 15.2 %copy-start.20 = (f32[1,1,1024]{2,1,0:T(1,128)S(1)}, f32[1,1,1024]{2,1,0:T(1,128)}, u32[]{:S(2)}) copy-start(f32[1,1,1024]{2,1,0:T(1,128)} %copy-done.19) | copy-start | bytes 12292
  186.5 15.2 %copy-start.22 = (f32[1,1,1024]{2,1,0:T(1,128)S(1)}, f32[1,1,1024]{2,1,0:T(1,128)}, u32[]{:S(2)}) copy-start(f32[1,1,1024]{2,1,0:T(1,128)} %copy-done.21) | copy-start | bytes 12292
  186.5 15.2 %copy-start.24 = (f32[512]{0:T(512)S(1)}, f32[512]{0:T(512)}, u32[]{:S(2)}) copy-start(f32[512]{0:T(512)} %copy-done.23) | copy-start | bytes 6148
  186.5 15.2 %copy-start.27 = (f32[512]{0:T(512)S(1)}, f32[512]{0:T(512)}, u32[]{:S(2)}) copy-start(f32[512]{0:T(512)} %copy-done.26) | copy-start | bytes 6148
  186.5 15.2 %copy-start.41 = (f32[1,1,1024]{2,1,0:T(1,128)S(1)}, f32[1,1,1024]{2,1,0:T(1,128)}, u32[]{:S(2)}) copy-start(f32[1,1,1024]{2,1,0:T(1,128)} %get-tuple-element.21) | copy-start | bytes 12292
  186.5 15.2 %copy-start.42 = (f32[1,1,1024]{2,1,0:T(1,128)S(1)}, f32[1,1,1024]{2,1,0:T(1,128)}, u32[]{:S(2)}) copy-start(f32[1,1,1024]{2,1,0:T(1,128)} %get-tuple-element.25) | copy-start | bytes 12292
  186.5 17.1 %copy-start.55 = (bf16[2048,1024]{1,0:T(8,128)(2,1)S(1)}, bf16[2048,1024]{1,0:T(8,128)(2,1)}, u32[]{:S(2)}) copy-start(bf16[2048,1024]{1,0:T(8,128)(2,1)} %param.26) | copy-start | bytes 12582916
  201.7 1.9 copy-start.5
  201.7 1.9 copy-start.16
  201.7 1.9 copy-start.29
  201.7 1.9 copy-start.34
  201.8 1.9 copy-start.37
  201.8 1.9 copy-start.44
  357.4 54.1 %copy-start.50 = (f32[1,1,1024]{2,1,0:T(1,128)S(1)}, f32[1,1,1024]{2,1,0:T(1,128)}, u32[]{:S(2)}) copy-start(f32[1,1,1024]{2,1,0:T(1,128)} %get-tuple-element.16) | copy-start | bytes 12292
  357.4 54.1 %copy-start.51 = (f32[1,1,1024]{2,1,0:T(1,128)S(1)}, f32[1,1,1024]{2,1,0:T(1,128)}, u32[]{:S(2)}) copy-start(f32[1,1,1024]{2,1,0:T(1,128)} %get-tuple-element.17) | copy-start | bytes 12292
  357.4 54.1 %copy-start.52 = (f32[1,1,1024]{2,1,0:T(1,128)S(1)}, f32[1,1,1024]{2,1,0:T(1,128)}, u32[]{:S(2)}) copy-start(f32[1,1,1024]{2,1,0:T(1,128)} %get-tuple-element.11) | copy-start | bytes 12292
  411.5 45.9 %copy-start.39 = (f32[1,1,1024]{2,1,0:T(1,128)S(1)}, f32[1,1,1024]{2,1,0:T(1,128)}, u32[]{:S(2)}) copy-start(f32[1,1,1024]{2,1,0:T(1,128)} %get-tuple-element.10) | copy-start | bytes 12292
  483.7 13.5 %copy-start.11 = (s32[8192]{0:T(1024)S(1)}, s32[8192]{0:T(1024)}, u32[]{:S(2)}) copy-start(s32[8192]{0:T(1024)} %param.20) | copy-start | bytes 98308
  483.7 13.5 %copy-start.46 = (pred[8192]{0:T(1024)(128)(4,1)S(1)}, pred[8192]{0:T(1024)(128)(4,1)}, u32[]{:S(2)}) copy-start(pred[8192]{0:T(1024)(128)(4,1)} %broadcast_compare_fusion) | copy-start | bytes 24580
  483.7 13.5 %copy-start.47 = (f32[1,1,1024]{2,1,0:T(1,128)S(1)}, f32[1,1,1024]{2,1,0:T(1,128)}, u32[]{:S(2)}) copy-start(f32[1,1,1024]{2,1,0:T(1,128)} %get-tuple-element.7) | copy-start | bytes 12292
  483.7 13.5 %copy-start.48 = (f32[1,1,1024]{2,1,0:T(1,128)S(1)}, f32[1,1,1024]{2,1,0:T(1,128)}, u32[]{:S(2)}) copy-start(f32[1,1,1024]{2,1,0:T(1,128)} %get-tuple-element.8) | copy-start | bytes 12292
  483.7 13.5 %copy-start.49 = (f32[1,1,1024]{2,1,0:T(1,128)S(1)}, f32[1,1,1024]{2,1,0:T(1,128)}, u32[]{:S(2)}) copy-start(f32[1,1,1024]{2,1,0:T(1,128)} %get-tuple-element.9) | copy-start | bytes 12292
  497.3 45.6 %copy-start.14 = (f32[1,1,1024]{2,1,0:T(1,128)S(1)}, f32[1,1,1024]{2,1,0:T(1,128)}, u32[]{:S(2)}) copy-start(f32[1,1,1024]{2,1,0:T(1,128)} %get-tuple-element.6) | copy-start | bytes 12292
  545.8 1.6 copy-start.6
  545.8 1.6 copy-start.17
  545.8 1.6 copy-start.30
  545.8 1.6 copy-start.31
  545.9 1.6 copy-start.32
  545.9 1.6 copy-start.35
  545.9 1.6 copy-start.38
  545.9 1.6 copy-start.45
  546.3 3.0 copy-start.1
where the time goes:
time: 554 us; the launch traced here: 550 us
  matrix products  207 us (37%)
  local copies, waits for them, and re-layouts  138 us (25%)
  waiting for transfers between devices  125 us (23%)
  other arithmetic  57.4 us (10%)
  starting transfers between devices  21.2 us (4%)
    all_to_all x1, waiting for transfers between devices, local_step(): lax.all_to_all(outgoing, 'graph', 0, 0, tiled=True)  125 us
    dot_general x6, matrix products, mlp_tail(): jnp.dot(hidden, w_out, preferred_element_type=jnp.float32)  70.5 us
    gather x1, local copies, waits for them, and re-layouts, mesh_step(): jnp.take(table_proj, edge_src, axis=0)  54.1 us
    dot_general x1, matrix products, mesh_step(): jnp.dot(edge_emb, w_edge_upd[:width], preferred_element_type=jnp.float32)  45.9 us
    dot_general x1, matrix products, mesh_step(): jnp.dot(aggregated, w_mesh_upd[width:], preferred_element_type=jnp.float32)  45.6 us
    gather x1, local copies, waits for them, and re-layouts, mesh_step(): jnp.take(mesh_proj, edge_dst, axis=0)  45.2 us
    gather x1, local copies, waits for them, and re-layouts, local_step(): outgoing = jnp.take(grid_emb, requests, axis=0)  35.3 us
    reduce_sum x6, other arithmetic, mlp_tail(): variance = jnp.mean(centered * centered, axis=-1, keepdims=True)  35.2 us
  transfers between devices with their start and end apart: 2, of which 1 were waited for; matrix products, arithmetic and copies ran while one was open for 24% of the time, Pallas kernels for 0%

commit v1 on v0

v1 whole, which is shorter than its diff:
```python
import functools

import jax
import jax.numpy as jnp
from jax import lax
from jax.experimental import pallas as pl
from jax.experimental.pallas import tpu as pltpu
from jax.sharding import PartitionSpec as P

LN_EPS = 1e-5
BF = jnp.bfloat16
F32 = jnp.float32
D = 1024
NODES = 512
EDGES = 8192
LANES = 128
SUB = 256
NC = 256
LN_ROWS = 32
ROWS1 = 1024
ROWS2 = 512
CHUNK = 4096


def silu(x):
    h = 0.5 * x
    return h + h * jnp.tanh(h)


def vec(vecs, mlp, k):
    return vecs[4 * mlp + k:4 * mlp + k + 1, :]


def layer_norm(x, gain, shift):
    mean = jnp.sum(x, axis=-1, keepdims=True) * (1.0 / D)
    c = x - mean
    var = jnp.sum(c * c, axis=-1, keepdims=True) * (1.0 / D)
    return c * lax.rsqrt(var + LN_EPS) * gain + shift


def first_layer(x, w, h, r0, bias=None):
    for n in range(D // NC):
        cols = slice(n * NC, (n + 1) * NC)
        pre = jnp.dot(x, w[:, cols], preferred_element_type=F32)
        if bias is not None:
            pre = pre + bias[:, cols]
        h[r0:r0 + SUB, cols] = silu(pre).astype(BF)


def second_layer(h, w, r, r0, bias):
    for n in range(D // NC):
        cols = slice(n * NC, (n + 1) * NC)
        r[r0:r0 + SUB, cols] = jnp.dot(h[r0:r0 + SUB, :], w[:, cols], preferred_element_type=F32) + bias[:, cols]


def norm_rows(r, r0, gain, shift, store):
    for q in range(0, SUB, LN_ROWS):
        store(r0 + q, layer_norm(r[r0 + q:r0 + q + LN_ROWS, :], gain, shift))


def embed_kernel(xe, a2, xg, a0, xm, a1, vecs, wsec, wedge, wgrid,
                 he_out, grid_out, hm_out, proj_out,
                 h, r, emb, wa, wb, wc, wd, we, wf, sems):
    i = pl.program_id(0)
    edge_steps = EDGES // ROWS1
    copies = [pltpu.make_async_copy(wsec.at[2], wa, sems.at[0]),
              pltpu.make_async_copy(wsec.at[0], wb, sems.at[1]),
              pltpu.make_async_copy(wgrid, wc, sems.at[2]),
              pltpu.make_async_copy(wsec.at[5], wd, sems.at[3]),
              pltpu.make_async_copy(wsec.at[1], we, sems.at[4]),
              pltpu.make_async_copy(wedge.at[pl.ds(2 * D, D)], wf, sems.at[5])]

    @pl.when(i == 0)
    def _():
        for c in copies:
            c.start()
        copies[0].wait()

    @pl.when(i < edge_steps)
    def _():
        blocks = range(0, ROWS1, SUB)
        for r0 in blocks:
            first_layer(xe[r0:r0 + SUB, :], a2, h, r0)
        for r0 in blocks:
            second_layer(h, wa, r, r0, vec(vecs, 2, 1))

            def store(row, y):
                he_out[row:row + LN_ROWS, :] = y.astype(BF)
            norm_rows(r, r0, vec(vecs, 2, 2), vec(vecs, 2, 3), store)

    blocks = range(0, NODES, SUB)

    @pl.when(i == edge_steps)
    def _():
        copies[1].wait()
        copies[2].wait()
        copies[3].wait()
        for r0 in blocks:
            first_layer(xg[r0:r0 + SUB, :], a0, h, r0)
        for r0 in blocks:
            second_layer(h, wb, r, r0, vec(vecs, 0, 1))

            def store(row, y):
                emb[row:row + LN_ROWS, :] = y.astype(BF)
            norm_rows(r, r0, vec(vecs, 0, 2), vec(vecs, 0, 3), store)
        for r0 in blocks:
            first_layer(emb[r0:r0 + SUB, :], wc, h, r0, vec(vecs, 5, 0))
        for r0 in blocks:
            second_layer(h, wd, r, r0, vec(vecs, 5, 1))

            def store_out(row, y):
                base = emb[row:row + LN_ROWS, :].astype(F32)
                grid_out[row:row + LN_ROWS, :] = (base + y).astype(BF)
            norm_rows(r, r0, vec(vecs, 5, 2), vec(vecs, 5, 3), store_out)

    @pl.when(i == edge_steps + 1)
    def _():
        copies[4].wait()
        copies[5].wait()
        for r0 in blocks:
            first_layer(xm[r0:r0 + SUB, :], a1, h, r0)
        for r0 in blocks:
            second_layer(h, we, r, r0, vec(vecs, 1, 1))

            def store(row, y):
                hm_out[row:row + LN_ROWS, :] = y.astype(BF)
            norm_rows(r, r0, vec(vecs, 1, 2), vec(vecs, 1, 3), store)
        for r0 in blocks:
            for n in range(D // NC):
                cols = slice(n * NC, (n + 1) * NC)
                p = jnp.dot(hm_out[r0:r0 + SUB, :], wf[:, cols], preferred_element_type=F32) + vec(vecs, 3, 0)[:, cols]
                for t in range(NC // LANES):
                    j = n * (NC // LANES) + t
                    proj_out[pl.ds(r0 * 8 + j, SUB, stride=8), :] = p[:, t * LANES:(t + 1) * LANES]


def edge_kernel(src_s, dst_s, need_s, he, dst_v, mask_v, a0, vecs, proj, hm, table, wsec, wedge, wmesh,
                mesh_out,
                ftab, stage, xg, gm, cat, h, r, new, acc, w0, w3, w12, sems):
    i = pl.program_id(0)
    steps = EDGES // ROWS2
    copies = [pltpu.make_async_copy(wsec.at[0], w0, sems.at[2]),
              pltpu.make_async_copy(wedge.at[pl.ds(0, 2 * D)], w12, sems.at[3]),
              pltpu.make_async_copy(wsec.at[3], w3, sems.at[4])]
    nchunk = table.shape[0] // CHUNK

    def stage_copy(c, slot):
        return pltpu.make_async_copy(table.at[pl.ds(pl.multiple_of(c * CHUNK, CHUNK), CHUNK)], stage.at[slot], sems.at[slot])

    def fetch_row(edge, row):
        s = src_s[edge]
        g = lax.shift_right_logical(s, 6) * 512 + need_s[s]
        xg[pl.ds(row, 1), :] = ftab[pl.ds(g, 1), :]

    @pl.when(i == 0)
    def _():
        stage_copy(0, 0).start()
        stage_copy(1, 1).start()
        for c in copies:
            c.start()

        def chunk(c, carry):
            slot = lax.rem(c, 2)
            stage_copy(c, slot).wait()

            def part(k, inner):
                rows = pl.multiple_of(k * 256, 256)
                ftab[pl.ds(pl.multiple_of(c * CHUNK + rows, 256), 256), :] = stage[slot, pl.ds(rows, 256), :].astype(F32)
                return inner
            lax.fori_loop(0, CHUNK // 256, part, 0)

            @pl.when(c + 2 < nchunk)
            def _():
                stage_copy(c + 2, slot).start()
            return carry
        lax.fori_loop(0, nchunk, chunk, 0)
        acc[...] = jnp.zeros_like(acc)

        def fetch8(k, carry):
            for t in range(8):
                fetch_row(k * 8 + t, k * 8 + t)
            return carry
        lax.fori_loop(0, ROWS2 // 8, fetch8, 0)
        for c in copies:
            c.wait()

    blocks = range(0, ROWS2, SUB)
    for r0 in blocks:
        first_layer(xg[r0:r0 + SUB, :].astype(BF), a0, h, r0)
    base = i * ROWS2
    after = jnp.minimum(i + 1, steps - 1) * ROWS2
    for e in range(ROWS2):
        d = dst_s[base + e]
        gm[e * 8:(e + 1) * 8, :] = proj[pl.ds(pl.multiple_of(d * 8, 8), 8), :]
        fetch_row(after + e, e)
    for r0 in blocks:
        cat[r0:r0 + SUB, :D] = he[r0:r0 + SUB, :]
        second_layer(h, w0, r, r0, vec(vecs, 0, 1))

        def store(row, y):
            cat[row:row + LN_ROWS, D:] = y.astype(BF)
        norm_rows(r, r0, vec(vecs, 0, 2), vec(vecs, 0, 3), store)
    for r0 in blocks:
        for n in range(D // NC):
            cols = slice(n * NC, (n + 1) * NC)
            pre = jnp.dot(cat[r0:r0 + SUB, :], w12[:, cols], preferred_element_type=F32)
            for t in range(NC // LANES):
                j = n * (NC // LANES) + t
                part = pre[:, t * LANES:(t + 1) * LANES] + gm[pl.ds(r0 * 8 + j, SUB, stride=8), :]
                h[r0:r0 + SUB, j * LANES:(j + 1) * LANES] = silu(part).astype(BF)
    for r0 in blocks:
        second_layer(h, w3, r, r0, vec(vecs, 3, 1))

        def store_new(row, y):
            new[row:row + LN_ROWS, :] = (he[row:row + LN_ROWS, :].astype(F32) + y).astype(BF)
        norm_rows(r, r0, vec(vecs, 3, 2), vec(vecs, 3, 3), store_new)
    for r0 in blocks:
        node = lax.broadcasted_iota(jnp.int32, (NODES, SUB), 0)
        dst = jnp.where(mask_v[0, :, r0:r0 + SUB] > 0, dst_v[0, :, r0:r0 + SUB], -1)
        inc = jnp.where(node == dst, 1.0, 0.0).astype(BF)
        for n in range(D // NC):
            cols = slice(n * NC, (n + 1) * NC)
            acc[:, cols] += jnp.dot(inc, new[r0:r0 + SUB, cols], preferred_element_type=F32)

    @pl.when(i == steps - 1)
    def _():
        last = [pltpu.make_async_copy(wmesh, w12, sems.at[3]),
                pltpu.make_async_copy(wsec.at[4], w0, sems.at[2])]
        for c in last:
            c.start()
        cat[:, :D] = hm[...]
        cat[:, D:] = acc[...].astype(BF)
        last[0].wait()
        for r0 in range(0, NODES, SUB):
            first_layer(cat[r0:r0 + SUB, :], w12, h, r0, vec(vecs, 4, 0))
        last[1].wait()
        for r0 in range(0, NODES, SUB):
            second_layer(h, w0, r, r0, vec(vecs, 4, 1))

            def store(row, y):
                mesh_out[row:row + LN_ROWS, :] = (hm[row:row + LN_ROWS, :].astype(F32) + y).astype(BF)
            norm_rows(r, r0, vec(vecs, 4, 2), vec(vecs, 4, 3), store)


def fixed(shape):
    return pl.BlockSpec(shape, lambda i, *_: (0,) * len(shape), pipeline_mode=pl.Buffered(1))


ANY = pl.BlockSpec(memory_space=pl.ANY)


def run_embed(xe, a2, xg, a0, xm, a1, vecs, w_second, w_edge_upd, w_grid_upd):
    steps = EDGES // ROWS1
    flops = 2 * D * (EDGES * (D + LANES) + NODES * (5 * D + 2 * LANES))
    wvm = pltpu.VMEM((D, D), BF)
    return pl.pallas_call(
        embed_kernel,
        grid=(steps + 2,),
        in_specs=[pl.BlockSpec((ROWS1, LANES), lambda i: (jnp.minimum(i, steps - 1), 0)), fixed((LANES, D)),
                  fixed((NODES, LANES)), fixed((LANES, D)), fixed((NODES, LANES)), fixed((LANES, D)),
                  fixed((24, D)), ANY, ANY, ANY],
        out_specs=[pl.BlockSpec((ROWS1, D), lambda i: (jnp.minimum(i, steps - 1), 0)),
                   fixed((NODES, D)), fixed((NODES, D)), fixed((NODES * 8, LANES))],
        out_shape=[jax.ShapeDtypeStruct((EDGES, D), BF), jax.ShapeDtypeStruct((NODES, D), BF),
                   jax.ShapeDtypeStruct((NODES, D), BF), jax.ShapeDtypeStruct((NODES * 8, LANES), F32)],
        scratch_shapes=[pltpu.VMEM((ROWS1, D), BF), pltpu.VMEM((ROWS1, D), F32), pltpu.VMEM((NODES, D), BF),
                        wvm, wvm, wvm, wvm, wvm, wvm, pltpu.SemaphoreType.DMA((6,))],
        compiler_params=pltpu.CompilerParams(vmem_limit_bytes=56 << 20, dimension_semantics=("arbitrary",)),
        cost_estimate=pl.CostEstimate(flops=flops, bytes_accessed=36 << 20, transcendentals=0),
        name="embed",
    )(xe, a2, xg, a0, xm, a1, vecs, w_second, w_edge_upd, w_grid_upd)


def run_edges(src, dst, need, he, mask, a0, vecs, proj, hm, table, w_second, w_edge_upd, w_mesh_upd):
    steps = EDGES // ROWS2
    flops = 2 * D * (EDGES * (4 * D + LANES + NODES) + NODES * 3 * D)
    lanes = lambda i, *_: (i, 0, 0)
    grid_spec = pltpu.PrefetchScalarGridSpec(
        num_scalar_prefetch=3,
        grid=(steps,),
        in_specs=[pl.BlockSpec((ROWS2, D), lambda i, *_: (i, 0)),
                  pl.BlockSpec((1, 1, ROWS2), lanes), pl.BlockSpec((1, 1, ROWS2), lanes),
                  fixed((LANES, D)), fixed((24, D)), fixed((NODES * 8, LANES)), fixed((NODES, D)),
                  ANY, ANY, ANY, ANY],
        out_specs=fixed((NODES, D)),
        scratch_shapes=[pltpu.VMEM(table.shape, F32), pltpu.VMEM((2, CHUNK, LANES), BF),
                        pltpu.VMEM((ROWS2, LANES), F32), pltpu.VMEM((ROWS2 * 8, LANES), F32),
                        pltpu.VMEM((ROWS2, 2 * D), BF), pltpu.VMEM((ROWS2, D), BF), pltpu.VMEM((ROWS2, D), F32),
                        pltpu.VMEM((ROWS2, D), BF), pltpu.VMEM((NODES, D), F32),
                        pltpu.VMEM((D, D), BF), pltpu.VMEM((D, D), BF), pltpu.VMEM((2 * D, D), BF),
                        pltpu.SemaphoreType.DMA((5,))])
    return pl.pallas_call(
        edge_kernel,
        grid_spec=grid_spec,
        out_shape=jax.ShapeDtypeStruct((NODES, D), BF),
        compiler_params=pltpu.CompilerParams(vmem_limit_bytes=67043328, dimension_semantics=("arbitrary",)),
        cost_estimate=pl.CostEstimate(flops=flops, bytes_accessed=48 << 20, transcendentals=0),
        name="edges",
    )(src, dst, need, he, dst.reshape(steps, 1, ROWS2), mask.reshape(steps, 1, ROWS2), a0, vecs, proj, hm, table,
      w_second, w_edge_upd, w_mesh_upd)


def pad_features(x):
    ones = jnp.ones((x.shape[0], 1), BF)
    return jnp.concatenate([x.astype(BF), ones, jnp.zeros((x.shape[0], LANES - 1 - x.shape[1]), BF)], axis=1)


def pad_weight(w, bias):
    return jnp.concatenate([w, bias[None, :], jnp.zeros((LANES - 1 - w.shape[0], w.shape[1]), BF)], axis=0)


def solution(mesh):
    sharded = P(('batch', 'graph'))
    replicated = P()

    def local_step(grid_feat, mesh_feat, edge_feat, need_rows, edge_src, edge_dst, edge_mask,
                   w_grid_emb, w_mesh_emb, w_edge_emb, w_edge_upd, w_mesh_upd, w_grid_upd, w_second, mlp_vecs):
        xg = pad_features(grid_feat)
        table = lax.all_gather(xg, 'graph', axis=0, tiled=True)
        a0 = pad_weight(w_grid_emb, mlp_vecs[0, 0])
        a1 = pad_weight(w_mesh_emb, mlp_vecs[1, 0])
        a2 = pad_weight(w_edge_emb, mlp_vecs[2, 0])
        vecs = mlp_vecs.astype(F32).reshape(24, D)
        he, grid_out, hm, proj = run_embed(pad_features(edge_feat), a2, xg, a0, pad_features(mesh_feat), a1, vecs,
                                           w_second, w_edge_upd, w_grid_upd)
        mesh_out = run_edges(edge_src, edge_dst, need_rows, he, edge_mask, a0, vecs, proj, hm, table,
                             w_second, w_edge_upd, w_mesh_upd)
        return mesh_out, grid_out

    return jax.shard_map(local_step, mesh=mesh,
                         in_specs=(sharded,) * 7 + (replicated,) * 8,
                         out_specs=(sharded, sharded), check_vma=False)
```

time: 554 us -> 239 us (0.43)
  the two profiles are of different devices: /device:TPU:37 before, /device:TPU:1 now
where the time goes in v1:
time: 239 us
  Pallas kernels  184 us (77%)
  waiting for transfers between devices  28.4 us (12%)
  between operations  14.1 us (6%)
  other arithmetic  7.9 us (3%)
  local copies, waits for them, and re-layouts  3.91 us (2%)
    pallas_call x1, Pallas kernels, run_edges(): pl.pallas_call(edge_kernel, grid_spec=grid_spec, out_shape=jax.ShapeDtype...  137 us
    pallas_call x1, Pallas kernels, run_embed(): pl.pallas_call(embed_kernel, grid=(steps + 2,), in_specs=[pl.BlockSpec((R...  46.9 us
    all_gather x1, waiting for transfers between devices, local_step(): table = lax.all_gather(xg, 'graph', axis=0, tiled=True)  28.4 us
  transfers between devices with their start and end apart: 1, of which 1 were waited for; matrix products, arithmetic and copies ran while one was open for 4% of the time, Pallas kernels for 20%

profile of v1, /device:TPU:1, one launch (start us, length us, event | category | flops | bytes accessed | tf_op | source)
XLA Modules:
  0.0 238.5 jit_solution(12175902304509095090)
XLA Ops:
  7.2 0.0 copy-start
  7.2 0.0 copy-start.1
  7.2 0.0 all-gather.2.cloned.1.call-start
  7.2 0.1 pad.11.clone
  7.3 0.1 pad.5.clone
  7.4 0.9 convert_element_type.11
  8.4 0.1 copy.21
  8.5 0.7 convert_element_type.12
  9.2 0.2 copy.22
  9.4 0.9 maximum_maximum_fusion.5
  10.2 0.0 all-gather.2.cloned.1.call-update
  10.3 0.1 pad.17.clone
  10.4 0.9 convert_element_type.10
  11.3 1.1 copy.20
  12.4 0.1 pad.16.clone
  12.4 1.4 reshape.20.vecs
  13.9 0.7 slice_bitcast_fusion
  14.6 1.5 maximum_maximum_fusion.3.a1
  16.1 0.0 copy-done
  16.1 0.0 copy-done.1
  16.1 0.9 maximum_maximum_fusion.1
  17.0 2.1 maximum_maximum_fusion.xe
  19.1 46.9 %embed.1 = (bf16[8192,1024]{1,0:T(8,128)(2,1)}, bf16[512,1024]{1,0:T(8,128)(2,1)}, bf16[512,1024]{1,0:T(8,128)(2,1)}, f32[4096,128]{1,0:T(8,128)}) custom-call(bf16[8192,128]{1,0:T(8,128)(2,1)} %maximum_maximum_fusion.xe, bf16[128,1024]{1,0:T(8,128)(2,1)} %get-tuple-element.15.a2, bf16[512,128]{1,0:T(8,128)(2,1)} %get-tuple-element.11.xg, ...), custom_call_target="tpu_custom_call" | custom-call | flops 24964497408 | bytes 37748736 | tf_op jit(solution)/shard_map/embed/pallas_call | solution.py:256
  66.0 28.4 %all-gather.2.cloned.1.call-done.table = bf16[65536,128]{1,0:T(8,128)(2,1)} async-done(((bf16[512,128]{1,0:T(8,128)(2,1)}), bf16[65536,128]{1,0:T(8,128)(2,1)}) %all-gather.2.cloned.1.call-update) | async-done | bytes 16777232 | tf_op jit(solution)/shard_map/all_gather | solution.py:319
  94.4 137.2 %edges.1 = bf16[512,1024]{1,0:T(8,128)(2,1)} custom-call(s32[8192]{0:T(1024)} %src_s.1, s32[8192]{0:T(1024)} %dst_s.1, s32[8192]{0:T(1024)} %need_s.1, bf16[8192,1024]{1,0:T(8,128)(2,1)} %get-tuple-element.6.he, s32[16,1,512]{2,1,0:T(1,128)} %bitcast.9, s32[16,1,512]{2,1,0:T(1,128)} %bitcast.10, bf16[128,1024]{1,0:T(8,128)(2,1)} %get-tuple-element.16.a0, ...), custom_call_target="tpu_custom_call" | custom-call | flops 82678120448 | bytes 50331648 | tf_op jit(solution)/shard_map/edges/pallas_call | solution.py:292
  (4 shorter events, 0.0 us)
Async XLA Ops:
  7.2 9.0 %copy-start = (bf16[102,1024]{1,0:T(8,128)(2,1)S(1)}, bf16[102,1024]{1,0:T(8,128)(2,1)}, u32[]{:S(2)}) copy-start(bf16[102,1024]{1,0:T(8,128)(2,1)} %param.22) | copy-start | bytes 626692
  7.2 8.9 %copy-start.1 = (bf16[4,1024]{1,0:T(4,128)(2,1)S(1)}, bf16[4,1024]{1,0:T(4,128)(2,1)}, u32[]{:S(2)}) copy-start(bf16[4,1024]{1,0:T(4,128)(2,1)} %param.24) | copy-start | bytes 24580
  7.2 87.2 %all-gather.2.cloned.1.call-start = ((), (), s32[]{:S(2)}) async-start(), calls=%async_computation | async-start | bytes 16908288 | tf_op jit(solution)/shard_map/all_gather | solution.py:319
Sparse Core Ops, SparseCore 0:
  11.1 83.2 all-gather.1

commit v2 on v0

v2 whole, which is shorter than its diff:
```python
import jax
import jax.numpy as jnp
from jax import lax
from jax.experimental import pallas as pl
from jax.experimental.pallas import tpu as pltpu
from jax.sharding import PartitionSpec as P

LN_EPS = 1e-5
BF = jnp.bfloat16
F32 = jnp.float32
D = 1024
NODES = 512
EDGES = 8192
LANES = 128
BAND = 512
NB = D // LANES
SUB = 256
NC = 256
LN_ROWS = 32
ROWS = 512
CHUNK = 4096


def silu_half(h):
    return h + h * jnp.tanh(h)


def vec(vecs, mlp, k):
    return vecs[mlp, k:k + 1, :]


def layer_norm(x, gain, shift):
    mean = jnp.sum(x, axis=-1, keepdims=True) * (1.0 / D)
    c = x - mean
    var = jnp.sum(c * c, axis=-1, keepdims=True) * (1.0 / D)
    return c * lax.rsqrt(var + LN_EPS) * gain + shift


def wide(*pieces):
    return jnp.concatenate(pieces, axis=1)


def lhs(ref, r0):
    return wide(*[ref[j, r0:r0 + SUB, :] for j in range(NB)])


def rhs(ref, n):
    return wide(ref[2 * n], ref[2 * n + 1])


def put(ref, n, r0, y):
    ref[2 * n, r0:r0 + SUB, :] = y[:, :LANES]
    ref[2 * n + 1, r0:r0 + SUB, :] = y[:, LANES:]


def put_rows(ref, row, y):
    for j in range(NB):
        ref[j, row:row + LN_ROWS, :] = y[:, j * LANES:(j + 1) * LANES]


def get_rows(ref, row):
    return wide(*[ref[j, row:row + LN_ROWS, :] for j in range(NB)])


def cols(n):
    return slice(n * NC, (n + 1) * NC)


def dot(a, b):
    return jnp.dot(a, b, preferred_element_type=F32)


def second_layer(h, w, r, r0, bias):
    a = lhs(h, r0)
    for n in range(D // NC):
        r[r0:r0 + SUB, cols(n)] = dot(a, rhs(w, n)) + bias[:, cols(n)]


def norm_rows(r, r0, vecs, mlp, store):
    for q in range(r0, r0 + SUB, LN_ROWS):
        store(q, layer_norm(r[q:q + LN_ROWS, :], vec(vecs, mlp, 2), vec(vecs, mlp, 3)))


def column_copies(src, dst, sem):
    return [pltpu.make_async_copy(src.at[:, pl.ds(j * LANES, LANES)], dst.at[j], sem) for j in range(NB)]


def start(copies):
    for c in copies:
        c.start()


def wait(copies):
    for c in copies:
        c.wait()


def narrow_weights(dst, w, bias):
    k = w.shape[0]
    dst[...] = jnp.zeros_like(dst)
    dst[0:k, :] = 0.5 * w[...].astype(F32)
    dst[k:k + 1, :] = 0.5 * bias


def narrow_layer(xt, w, h, r0):
    x = xt[:, r0:r0 + SUB].T.astype(BF)
    for n in range(D // NC):
        put(h, n, r0, silu_half(dot(x, w[:, cols(n)].astype(BF))).astype(BF))


def grid_weights(dst, tmp, w, bias):
    k = w.shape[0]
    tmp[0:LANES, :] = jnp.zeros((LANES, D), F32)
    tmp[0:k, :] = 0.5 * w[...].astype(F32)
    tmp[k:k + 1, :] = 0.5 * bias
    for j in range(NB):
        dst[j] = tmp[0:LANES, j * LANES:(j + 1) * LANES].astype(BF)


def grid_layer(x, w, h, r0):
    for n in range(D // NC):
        put(h, n, r0, silu_half(dot(x, rhs(w, n))).astype(BF))


def full_layer(a, w, h, r0, bias):
    for n in range(D // NC):
        pre = dot(a, rhs(w, n)) + bias[:, cols(n)]
        put(h, n, r0, silu_half(0.5 * pre).astype(BF))


def embed_kernel(ef, mf, w_edge, w_mesh, vecs, wsec, wedge, he_out, hm_out, proj_out,
                 xt, a1, a2, h, r, b1, b2, w3, sems):
    i = pl.program_id(0)
    c1 = column_copies(wsec.at[1], b1, sems.at[0])
    c3 = column_copies(wedge.at[pl.ds(2 * D, D)], w3, sems.at[1])
    c2 = column_copies(wsec.at[2], b2, sems.at[2])
    blocks = range(0, ROWS, SUB)

    @pl.when(i == 0)
    def _():
        start(c1)
        start(c3)
        start(c2)
        narrow_weights(a1, w_mesh, vec(vecs, 1, 0))
        narrow_weights(a2, w_edge, vec(vecs, 2, 0))
        k = mf.shape[0]
        xt[...] = jnp.ones_like(xt)
        xt[0:k, :] = mf[...]
        for r0 in blocks:
            narrow_layer(xt, a1, h, r0)
        wait(c1)
        for r0 in blocks:
            second_layer(h, b1, r, r0, vec(vecs, 1, 1))
            norm_rows(r, r0, vecs, 1, lambda row, y: put_rows(hm_out, row, y.astype(BF)))
        wait(c3)
        for r0 in blocks:
            a = lhs(hm_out, r0)
            for n in range(D // NC):
                p = dot(a, rhs(w3, n)) + vec(vecs, 3, 0)[:, cols(n)]
                for t in range(2):
                    proj_out[pl.ds(r0 * 8 + 2 * n + t, SUB, stride=8), :] = p[:, t * LANES:(t + 1) * LANES]
        xt[...] = jnp.ones_like(xt)
        wait(c2)

    @pl.when(i > 0)
    def _():
        xt[0:ef.shape[0], :] = ef[...]
        for r0 in blocks:
            narrow_layer(xt, a2, h, r0)
        for r0 in blocks:
            second_layer(h, b2, r, r0, vec(vecs, 2, 1))
            norm_rows(r, r0, vecs, 2, lambda row, y: put_rows(he_out, row, y.astype(BF)))


def project_kernel(dst_s, he, proj, xg, w_grid, vecs, wedge, wsec, wgrid, pre_out, grid_out,
                   ga, gb, a0, emb, h, r, w1, b0, wg, b5, sems):
    i = pl.program_id(0)
    steps = EDGES // (2 * ROWS)
    c1 = column_copies(wedge.at[pl.ds(0, D)], w1, sems.at[0])
    c0 = column_copies(wsec.at[0], b0, sems.at[1])
    cg = column_copies(wgrid, wg, sems.at[2])
    c5 = column_copies(wsec.at[5], b5, sems.at[3])

    def fetch(buf, edge, row):
        d = dst_s[edge]
        buf[pl.ds(pl.multiple_of(row * 8, 8), 8), :] = proj[pl.ds(pl.multiple_of(d * 8, 8), 8), :]

    @pl.when(i == 0)
    def _():
        start(c1)
        start(c0)
        start(cg)
        start(c5)

        def fetch8(k, carry):
            for t in range(8):
                fetch(ga, k * 8 + t, k * 8 + t)
            return carry
        lax.fori_loop(0, ROWS // 8, fetch8, 0)
        wait(c1)

    @pl.when(i < steps)
    def _():
        base = i * (2 * ROWS)
        for half, (buf, other) in enumerate(((ga, gb), (gb, ga))):
            nxt = jnp.minimum(base + (half + 1) * ROWS, EDGES - ROWS)
            for e in range(ROWS):
                fetch(other, nxt + e, e)
            for r0 in range(0, ROWS, SUB):
                a = lhs(he, half * ROWS + r0)
                for n in range(D // NC):
                    p = dot(a, rhs(w1, n))
                    for t in range(2):
                        j = 2 * n + t
                        pre_out[half * ROWS + r0:half * ROWS + r0 + SUB, j * LANES:(j + 1) * LANES] = (
                            p[:, t * LANES:(t + 1) * LANES] + buf[pl.ds(r0 * 8 + j, SUB, stride=8), :])

    @pl.when(i == steps)
    def _():
        blocks = range(0, BAND, SUB)
        grid_weights(a0, r, w_grid, vec(vecs, 0, 0))
        wait(c0)
        wait(cg)
        wait(c5)
        for r0 in blocks:
            grid_layer(xg[r0:r0 + SUB, :], a0, h, r0)
        for r0 in blocks:
            second_layer(h, b0, r, r0, vec(vecs, 0, 1))
            norm_rows(r, r0, vecs, 0, lambda row, y: put_rows(emb, row, y.astype(BF)))
        for r0 in blocks:
            full_layer(lhs(emb, r0), wg, h, r0, vec(vecs, 5, 0))
        for r0 in blocks:
            second_layer(h, b5, r, r0, vec(vecs, 5, 1))

            def store(row, y):
                grid_out[row:row + LN_ROWS, :] = (get_rows(emb, row).astype(F32) + y).astype(BF)
            norm_rows(r, r0, vecs, 5, store)


def edge_kernel(src_s, need_s, par_s, he, pre, dst_v, mask_v, dst_p, mask_p, w_grid, vecs, hm, own, swapped,
                wsec, wedge, wmesh, mesh_out,
                ftab, stage, xg, a0, h, r, hg, newx, newy, acc, b0, b3, w2, wm, sems):
    i = pl.program_id(0)
    steps = EDGES // ROWS
    c0 = column_copies(wsec.at[0], b0, sems.at[2])
    c2 = column_copies(wedge.at[pl.ds(D, D)], w2, sems.at[3])
    c3 = column_copies(wsec.at[3], b3, sems.at[4])
    cm = column_copies(wmesh, wm, sems.at[5])
    c4 = column_copies(wsec.at[4], b0, sems.at[6])
    per = own.shape[0] // CHUNK

    def stage_copy(c):
        src = own if c < per else swapped
        return pltpu.make_async_copy(src.at[pl.ds((c % per) * CHUNK, CHUNK)], stage.at[c % 2], sems.at[c % 2])

    def fetch_row(edge, row):
        s = src_s[edge]
        g = lax.shift_right_logical(s, 6) * BAND + need_s[s]
        xg[pl.ds(row, 1), :] = ftab[pl.ds(g, 1), :]

    @pl.when(i == 0)
    def _():
        stage_copy(0).start()
        stage_copy(1).start()
        start(c0)
        start(c2)
        start(c3)
        parity = par_s[0]
        grid_weights(a0, r, w_grid, vec(vecs, 0, 0))
        acc[...] = jnp.zeros_like(acc)
        newy[...] = jnp.zeros_like(newy)
        for c in range(2 * per):
            stage_copy(c).wait()
            owner = parity if c < per else 1 - parity

            def part(k, carry):
                band = 2 * ((c % per) * (CHUNK // BAND) + k) + owner
                for half in range(2):
                    piece = stage[c % 2, pl.ds(pl.multiple_of(k * BAND + half * 256, 256), 256), :]
                    ftab[pl.ds(pl.multiple_of(band * BAND + half * 256, 256), 256), :] = piece.astype(F32)
                return carry
            lax.fori_loop(0, CHUNK // BAND, part, 0)
            if c + 2 < 2 * per:
                stage_copy(c + 2).start()
        start(cm)

        def fetch8(k, carry):
            for t in range(8):
                fetch_row(k * 8 + t, k * 8 + t)
            return carry
        lax.fori_loop(0, ROWS // 8, fetch8, 0)
        wait(c0)
        wait(c2)
        wait(c3)

    def aggregate(dst_ref, mask_ref, r0, new):
        node = lax.broadcasted_iota(jnp.int32, (NODES, SUB), 0)
        dst = jnp.where(mask_ref[0, :, r0:r0 + SUB] > 0, dst_ref[0, :, r0:r0 + SUB], -1)
        inc = jnp.where(node == dst, 1.0, 0.0).astype(BF)
        for n in range(D // NC):
            acc[:, cols(n)] += dot(inc, rhs(new, n))

    def update(r0, new):
        second_layer(h, b3, r, r0, vec(vecs, 3, 1))

        def store(row, y):
            put_rows(new, row - r0, (get_rows(he, row).astype(F32) + y).astype(BF))
        norm_rows(r, r0, vecs, 3, store)

    blocks = range(0, ROWS, SUB)
    for r0 in blocks:
        grid_layer(xg[r0:r0 + SUB, :].astype(BF), a0, h, r0)
    after = jnp.minimum(i + 1, steps - 1) * ROWS
    for e in range(ROWS):
        fetch_row(after + e, e)
    for r0 in blocks:
        second_layer(h, b0, r, r0, vec(vecs, 0, 1))
        norm_rows(r, r0, vecs, 0, lambda row, y: put_rows(hg, row, y.astype(BF)))
    for r0 in blocks:
        a = lhs(hg, r0)
        for n in range(D // NC):
            x = dot(a, rhs(w2, n)) + pre[r0:r0 + SUB, cols(n)]
            put(h, n, r0, silu_half(0.5 * x).astype(BF))
    update(0, newx)
    aggregate(dst_p, mask_p, SUB, newy)
    update(SUB, newy)
    aggregate(dst_v, mask_v, 0, newx)

    @pl.when(i == steps - 1)
    def _():
        start(c4)
        aggregate(dst_v, mask_v, SUB, newy)
        for j in range(NB):
            hg[j] = acc[:, j * LANES:(j + 1) * LANES].astype(BF)
        wait(cm)
        for r0 in range(0, NODES, SUB):
            full_layer(wide(lhs(hm, r0), lhs(hg, r0)), wm, h, r0, vec(vecs, 4, 0))
        wait(c4)
        for r0 in range(0, NODES, SUB):
            second_layer(h, b0, r, r0, vec(vecs, 4, 1))

            def store(row, y):
                mesh_out[row:row + LN_ROWS, :] = (get_rows(hm, row).astype(F32) + y).astype(BF)
            norm_rows(r, r0, vecs, 4, store)


def fixed(shape):
    return pl.BlockSpec(shape, lambda i, *_: (0,) * len(shape), pipeline_mode=pl.Buffered(1))


ANY = pl.BlockSpec(memory_space=pl.ANY)
SQUARE = pltpu.VMEM((NB, D, LANES), BF)
HIDDEN = pltpu.VMEM((NB, ROWS, LANES), BF)
RESULT = pltpu.VMEM((ROWS, D), F32)
VECS = (6, 4, D)


def params(limit):
    return pltpu.CompilerParams(vmem_limit_bytes=limit, dimension_semantics=("arbitrary",))


def cost(macs, size):
    return pl.CostEstimate(flops=2 * macs, bytes_accessed=size, transcendentals=0)


def run_embed(edge_t, mesh_t, w_edge_emb, w_mesh_emb, vecs, w_second, w_edge_upd):
    steps = EDGES // ROWS
    before = lambda i: jnp.maximum(i - 1, 0)
    return pl.pallas_call(
        embed_kernel,
        grid=(steps + 1,),
        in_specs=[pl.BlockSpec((edge_t.shape[0], ROWS), lambda i: (0, before(i))), fixed(mesh_t.shape),
                  fixed(w_edge_emb.shape), fixed(w_mesh_emb.shape), fixed(VECS), ANY, ANY],
        out_specs=[pl.BlockSpec((NB, ROWS, LANES), lambda i: (0, before(i), 0)),
                   fixed((NB, NODES, LANES)), fixed((NODES * 8, LANES))],
        out_shape=[jax.ShapeDtypeStruct((NB, EDGES, LANES), BF), jax.ShapeDtypeStruct((NB, NODES, LANES), BF),
                   jax.ShapeDtypeStruct((NODES * 8, LANES), F32)],
        scratch_shapes=[pltpu.VMEM((8, ROWS), F32), pltpu.VMEM((8, D), F32), pltpu.VMEM((8, D), F32), HIDDEN, RESULT,
                        SQUARE, SQUARE, SQUARE, pltpu.SemaphoreType.DMA((3,))],
        compiler_params=params(40 << 20),
        cost_estimate=cost(EDGES * D * (D + 256) + NODES * D * (2 * D + 256), 26 << 20),
        name="embed",
    )(edge_t, mesh_t, w_edge_emb, w_mesh_emb, vecs, w_second, w_edge_upd)


def run_project(dst, he, proj, xg, w_grid_emb, vecs, w_edge_upd, w_second, w_grid_upd):
    steps = EDGES // (2 * ROWS)
    block = lambda i: jnp.minimum(i, steps - 1)
    grid_spec = pltpu.PrefetchScalarGridSpec(
        num_scalar_prefetch=1,
        grid=(steps + 1,),
        in_specs=[pl.BlockSpec((NB, 2 * ROWS, LANES), lambda i, *_: (0, block(i), 0)), fixed((NODES * 8, LANES)),
                  fixed((BAND, LANES)), fixed(w_grid_emb.shape), fixed(VECS), ANY, ANY, ANY],
        out_specs=[pl.BlockSpec((2 * ROWS, D), lambda i, *_: (block(i), 0)), fixed((BAND, D))],
        scratch_shapes=[pltpu.VMEM((ROWS * 8, LANES), F32), pltpu.VMEM((ROWS * 8, LANES), F32),
                        pltpu.VMEM((NB, LANES, LANES), BF), HIDDEN, HIDDEN, RESULT,
                        SQUARE, SQUARE, SQUARE, SQUARE, pltpu.SemaphoreType.DMA((4,))])
    return pl.pallas_call(
        project_kernel,
        grid_spec=grid_spec,
        out_shape=[jax.ShapeDtypeStruct((EDGES, D), F32), jax.ShapeDtypeStruct((BAND, D), BF)],
        compiler_params=params(48 << 20),
        cost_estimate=cost(EDGES * D * D + BAND * D * (3 * D + 256), 58 << 20),
        name="project",
    )(dst, he, proj, xg, w_grid_emb, vecs, w_edge_upd, w_second, w_grid_upd)


def run_edges(src, need, parity, he, pre, dst, mask, w_grid_emb, vecs, hm, own, swapped, w_second, w_edge_upd, w_mesh_upd):
    steps = EDGES // ROWS
    here = pl.BlockSpec((1, 1, ROWS), lambda i, *_: (i, 0, 0))
    before = pl.BlockSpec((1, 1, ROWS), lambda i, *_: (jnp.maximum(i - 1, 0), 0, 0))
    grid_spec = pltpu.PrefetchScalarGridSpec(
        num_scalar_prefetch=3,
        grid=(steps,),
        in_specs=[pl.BlockSpec((NB, ROWS, LANES), lambda i, *_: (0, i, 0)), pl.BlockSpec((ROWS, D), lambda i, *_: (i, 0)),
                  here, here, before, before, fixed(w_grid_emb.shape), fixed(VECS), fixed((NB, NODES, LANES)),
                  ANY, ANY, ANY, ANY, ANY],
        out_specs=fixed((NODES, D)),
        scratch_shapes=[pltpu.VMEM((2 * own.shape[0], LANES), F32), pltpu.VMEM((2, CHUNK, LANES), BF),
                        pltpu.VMEM((ROWS, LANES), F32), pltpu.VMEM((NB, LANES, LANES), BF), HIDDEN, RESULT, HIDDEN,
                        pltpu.VMEM((NB, SUB, LANES), BF), pltpu.VMEM((NB, SUB, LANES), BF), pltpu.VMEM((NODES, D), F32),
                        SQUARE, SQUARE, SQUARE, pltpu.VMEM((NB, 2 * D, LANES), BF),
                        pltpu.SemaphoreType.DMA((7,))])
    dst = dst.reshape(steps, 1, ROWS)
    mask = mask.reshape(steps, 1, ROWS)
    return pl.pallas_call(
        edge_kernel,
        grid_spec=grid_spec,
        out_shape=jax.ShapeDtypeStruct((NODES, D), BF),
        compiler_params=params(67043328),
        cost_estimate=cost(EDGES * D * (3 * D + 256 + NODES) + NODES * 3 * D * D, 80 << 20),
        name="edges",
    )(src, need, parity, he, pre, dst, mask, dst, mask, w_grid_emb, vecs, hm, own, swapped, w_second, w_edge_upd, w_mesh_upd)


def pad_features(x):
    ones = jnp.ones((x.shape[0], 1), BF)
    return jnp.concatenate([x.astype(BF), ones, jnp.zeros((x.shape[0], LANES - 1 - x.shape[1]), BF)], axis=1)


def gather_own(xg, size):
    return lax.all_gather(xg, 'graph', axis=0, tiled=True,
                          axis_index_groups=[list(range(0, size, 2)), list(range(1, size, 2))])


def swap_halves(own, size):
    swapped = lax.ppermute(own, 'graph', [(k, k ^ 1) for k in range(size)])
    return swapped, lax.rem(lax.axis_index('graph'), 2).astype(jnp.int32).reshape(1)


def solution(mesh):
    size = mesh.shape['graph']
    sharded = P(('batch', 'graph'))
    replicated = P()

    def local_step(grid_feat, mesh_feat, edge_feat, need_rows, edge_src, edge_dst, edge_mask,
                   w_grid_emb, w_mesh_emb, w_edge_emb, w_edge_upd, w_mesh_upd, w_grid_upd, w_second, mlp_vecs):
        xg = pad_features(grid_feat)
        own = gather_own(xg, size)
        vecs = mlp_vecs.astype(F32)
        he, hm, proj = run_embed(edge_feat.T, mesh_feat.T, w_edge_emb, w_mesh_emb, vecs, w_second, w_edge_upd)
        own, he = lax.optimization_barrier((own, he))
        swapped, parity = swap_halves(own, size)
        pre, grid_out = run_project(edge_dst, he, proj, xg, w_grid_emb, vecs, w_edge_upd, w_second, w_grid_upd)
        mesh_out = run_edges(edge_src, need_rows, parity, he, pre, edge_dst, edge_mask, w_grid_emb, vecs, hm, own, swapped,
                             w_second, w_edge_upd, w_mesh_upd)
        return mesh_out, grid_out

    return jax.shard_map(local_step, mesh=mesh,
                         in_specs=(sharded,) * 7 + (replicated,) * 8,
                         out_specs=(sharded, sharded), check_vma=False)
```

time: 554 us -> 246 us (0.44)
  the two profiles are of different devices: /device:TPU:37 before, /device:TPU:1 now
where the time goes in v2:
time: 246 us; the launch traced here: 245 us
  Pallas kernels  180 us (73%)
  waiting for transfers between devices  36.8 us (15%)
  between operations  14.1 us (6%)
  local copies, waits for them, and re-layouts  10 us (4%)
  other arithmetic  2.46 us (1%)
    pallas_call x1, Pallas kernels, run_edges(): pl.pallas_call(edge_kernel, grid_spec=grid_spec, out_shape=jax.ShapeDtype...  107 us
    pallas_call x1, Pallas kernels, run_embed(): pl.pallas_call(embed_kernel, grid=(steps + 1,), in_specs=[pl.BlockSpec((e...  37.6 us
    all_gather x1, waiting for transfers between devices, gather_own(): lax.all_gather(xg, 'graph', axis=0, tiled=True, axis_index_groups=[list(r...  36.8 us
    pallas_call x1, Pallas kernels, run_project(): pl.pallas_call(project_kernel, grid_spec=grid_spec, out_shape=[jax.ShapeD...  35.4 us
    unnamed x26, local copies, waits for them, and re-layouts  9.72 us
  transfers between devices with their start and end apart: 2, of which 1 were waited for; matrix products, arithmetic and copies ran while one was open for 0% of the time, Pallas kernels for 30%

profile of v2, /device:TPU:1, one launch (start us, length us, event | category | flops | bytes accessed | tf_op | source)
XLA Modules:
  0.0 244.8 jit_solution(7645898325059771083)
XLA Ops:
  7.2 0.0 all-gather.2.cloned.1.call-start
  7.2 0.9 convert_element_type.6
  8.2 0.1 copy.18
  8.3 0.1 pad.2.clone
  8.4 0.1 pad.1.clone
  8.5 0.7 maximum_maximum_fusion.xg
  9.2 0.0 all-gather.2.cloned.1.call-update
  9.2 0.8 convert_element_type.7.vecs
  10.0 0.0 copy-start.1
  10.0 0.0 copy-start.2
  10.0 2.8 %copy-done.2 = bf16[3072,1024]{1,0:T(8,128)(2,1)S(1)} copy-done((bf16[3072,1024]{1,0:T(8,128)(2,1)S(1)}, bf16[3072,1024]{1,0:T(8,128)(2,1)}, u32[]{:S(2)}) %copy-start.2) | copy-done | bytes 6291480
  12.8 0.0 copy-start.5
  12.8 0.9 copy-done.5
  13.7 0.0 copy-start.7
  13.7 0.7 copy-done.7
  14.4 0.0 copy-start.8
  14.4 0.7 copy-done.8
  15.1 0.0 copy-start.9
  15.1 0.7 copy-done.9
  15.8 0.0 copy-start
  15.8 0.0 copy-start.3
  15.8 0.0 copy-start.4
  15.8 0.0 copy-start.6
  15.8 37.6 %embed.1 = (bf16[8,8192,128]{2,1,0:T(8,128)(2,1)}, bf16[8,512,128]{2,1,0:T(8,128)(2,1)S(1)}, f32[4096,128]{1,0:T(8,128)S(1)}) custom-call(f32[4,8192]{1,0:T(4,128)S(1)} %bitcast.6, f32[3,512]{1,0:T(4,128)S(1)} %bitcast.9, bf16[4,1024]{1,0:T(4,128)(2,1)S(1)} %copy-done.8, bf16[3,1024]{1,0:T(4,128)(2,1)S(1)} %copy-done.9, ...), custom_call_target="tpu_custom_call" | custom-call | flops 23890755584 | bytes 27262976 | tf_op jit(solution)/shard_map/embed/pallas_call | solution.py:369
  53.5 0.0 copy-start.10
  53.5 1.3 copy-done.10
  54.8 0.0 copy-start.12
  54.8 1.0 copy-done.12
  55.8 36.8 %all-gather.2.cloned.1.call-done.own = bf16[32768,128]{1,0:T(8,128)(2,1)} async-done(((bf16[512,128]{1,0:T(8,128)(2,1)}), bf16[32768,128]{1,0:T(8,128)(2,1)}) %all-gather.2.cloned.1.call-update) | async-done | bytes 8388624 | tf_op jit(solution)/shard_map/all_gather | solution.py:442
  92.6 0.9 collective-permute-start
  93.5 0.0 copy-done.1
  93.5 0.0 copy-done
  93.5 0.0 copy-done.3
  93.5 0.0 copy-done.4
  93.5 0.0 copy-done.6
  93.5 0.0 copy-start.11
  93.5 1.6 copy-done.11
  95.1 35.4 %project.1 = (f32[8192,1024]{1,0:T(8,128)}, bf16[512,1024]{1,0:T(8,128)(2,1)}) custom-call(s32[8192]{0:T(1024)S(1)} %copy-done.6, bf16[8,8192,128]{2,1,0:T(8,128)(2,1)} %get-tuple-element.10.he, f32[4096,128]{1,0:T(8,128)S(1)} %copy-done.11, bf16[512,128]{1,0:T(8,128)(2,1)S(1)} %copy-done, bf16[102,1024]{1,0:T(8,128)(2,1)S(1)} %copy-done.4, ...), custom_call_target="tpu_custom_call" | custom-call | flops 20669530112 | bytes 60817408 | tf_op jit(solution)/shard_map/project/pallas_call | solution.py:398
  130.6 0.0 collective-permute-done.swapped
  130.6 107.3 %edges.1 = bf16[512,1024]{1,0:T(8,128)(2,1)} custom-call(s32[8192]{0:T(1024)} %src_s.1, s32[8192]{0:T(1024)} %need_s.1, s32[1]{0:T(128)} %bitcast.par_s, bf16[8,8192,128]{2,1,0:T(8,128)(2,1)} %get-tuple-element.10.he, f32[8192,1024]{1,0:T(8,128)} %get-tuple-element.12.pre, s32[16,1,512]{2,1,0:T(1,128)} %bitcast.7, s32[16,1,512]{2,1,0:T(1,128)} %bitcast.10, ...), custom_call_target="tpu_custom_call" | custom-call | flops 67645734912 | bytes 83886080 | tf_op jit(solution)/shard_map/edges/pallas_call | solution.py:426
  (1 shorter events, 0.0 us)
Async XLA Ops:
  7.2 85.4 %all-gather.2.cloned.1.call-start = ((), (), s32[]{:S(2)}) async-start(), calls=%async_computation | async-start | bytes 8519680 | tf_op jit(solution)/shard_map/all_gather | solution.py:442
  10.0 83.5 %copy-start.1 = (f32[6,4,1024]{2,1,0:T(4,128)}, f32[6,4,1024]{2,1,0:T(4,128)S(1)}, u32[]{:S(2)}) copy-start(f32[6,4,1024]{2,1,0:T(4,128)S(1)} %convert_element_type.7.vecs) | copy-start | bytes 294916
  10.0 2.8 %copy-start.2 = (bf16[3072,1024]{1,0:T(8,128)(2,1)S(1)}, bf16[3072,1024]{1,0:T(8,128)(2,1)}, u32[]{:S(2)}) copy-start(bf16[3072,1024]{1,0:T(8,128)(2,1)} %wedge.5) | copy-start | bytes 18874372
  12.8 0.9 copy-start.5
  13.7 0.7 copy-start.7
  14.4 0.7 copy-start.8
  15.1 0.7 copy-start.9
  15.8 77.7 %copy-start = (bf16[512,128]{1,0:T(8,128)(2,1)S(1)}, bf16[512,128]{1,0:T(8,128)(2,1)}, u32[]{:S(2)}) copy-start(bf16[512,128]{1,0:T(8,128)(2,1)} %maximum_maximum_fusion.xg) | copy-start | bytes 393220
  15.8 77.7 %copy-start.3 = (bf16[1024,1024]{1,0:T(8,128)(2,1)S(1)}, bf16[1024,1024]{1,0:T(8,128)(2,1)}, u32[]{:S(2)}) copy-start(bf16[1024,1024]{1,0:T(8,128)(2,1)} %wgrid.1) | copy-start | bytes 6291460
  15.8 77.7 %copy-start.4 = (bf16[102,1024]{1,0:T(8,128)(2,1)S(1)}, bf16[102,1024]{1,0:T(8,128)(2,1)}, u32[]{:S(2)}) copy-start(bf16[102,1024]{1,0:T(8,128)(2,1)} %w_grid.3) | copy-start | bytes 626692
  15.8 77.7 %copy-start.6 = (s32[8192]{0:T(1024)S(1)}, s32[8192]{0:T(1024)}, u32[]{:S(2)}) copy-start(s32[8192]{0:T(1024)} %dst_s.1) | copy-start | bytes 98308
  53.5 1.3 copy-start.10
  54.8 1.0 copy-start.12
  92.6 38.0 %collective-permute-start = (bf16[32768,128]{1,0:T(8,128)(2,1)}, bf16[32768,128]{1,0:T(8,128)(2,1)}, u32[]{:S(2)}, u32[]{:S(2)}) collective-permute-start(bf16[32768,128]{1,0:T(8,128)(2,1)} %all-gather.2.cloned.1.call-done.own), channel_id=1, source_target_pairs={{0,1},{1,0},{2,3},{3,2},{4,5},{5,4},{6,7},{7,6},{8,9},{9,8},{10,11... | collective-permute-start | bytes 25165832 | tf_op jit(solution)/shard_map/ppermute | solution.py:447
  93.5 1.6 copy-start.11
Sparse Core Ops, SparseCore 0:
  11.4 81.1 all-gather.1

commit v3 on v0

v3 whole, which is shorter than its diff:
```python
import jax
import jax.numpy as jnp
from jax import lax
from jax.experimental import pallas as pl
from jax.experimental.pallas import tpu as pltpu
from jax.sharding import PartitionSpec as P

LN_EPS = 1e-5
BF = jnp.bfloat16
F32 = jnp.float32
D = 1024
NODES = 512
EDGES = 8192
LANES = 128
BAND = 512
NB = D // LANES
SUB = 256
NC = 256
LN_ROWS = 32
ROWS = 512
ROWS_E = 2048
PICK = 1024


def silu_half(h):
    return h + h * jnp.tanh(h)


def vec(vecs, mlp, k):
    return vecs[mlp, k:k + 1, :]


def layer_norm(x, gain, shift):
    mean = jnp.sum(x, axis=-1, keepdims=True) * (1.0 / D)
    c = x - mean
    var = jnp.sum(c * c, axis=-1, keepdims=True) * (1.0 / D)
    return c * lax.rsqrt(var + LN_EPS) * gain + shift


def wide(*pieces):
    return jnp.concatenate(pieces, axis=1)


def lhs(ref, r0):
    return wide(*[ref[j, r0:r0 + SUB, :] for j in range(NB)])


def rhs(ref, n):
    return wide(ref[2 * n], ref[2 * n + 1])


def put(ref, n, r0, y):
    ref[2 * n, r0:r0 + SUB, :] = y[:, :LANES]
    ref[2 * n + 1, r0:r0 + SUB, :] = y[:, LANES:]


def put_rows(ref, row, y):
    for j in range(NB):
        ref[j, row:row + LN_ROWS, :] = y[:, j * LANES:(j + 1) * LANES]


def get_rows(ref, row):
    return wide(*[ref[j, row:row + LN_ROWS, :] for j in range(NB)])


def cols(n):
    return slice(n * NC, (n + 1) * NC)


def dot(a, b):
    return jnp.dot(a, b, preferred_element_type=F32)


def second_layer(h, w, r, r0, bias):
    a = lhs(h, r0)
    for n in range(D // NC):
        r[r0:r0 + SUB, cols(n)] = dot(a, rhs(w, n)) + bias[:, cols(n)]


def norm_rows(r, r0, vecs, mlp, store):
    for q in range(r0, r0 + SUB, LN_ROWS):
        store(q, layer_norm(r[q:q + LN_ROWS, :], vec(vecs, mlp, 2), vec(vecs, mlp, 3)))


def column_copies(src, dst, sem):
    return [pltpu.make_async_copy(src.at[:, pl.ds(j * LANES, LANES)], dst.at[j], sem) for j in range(NB)]


def start(copies):
    for c in copies:
        c.start()


def wait(copies):
    for c in copies:
        c.wait()


def narrow_weights(dst, w, bias):
    k = w.shape[0]
    dst[...] = jnp.zeros_like(dst)
    dst[0:k, :] = 0.5 * w[...].astype(F32)
    dst[k:k + 1, :] = 0.5 * bias


def narrow_layer(xt, w, h, r0):
    x = xt[:, r0:r0 + SUB].T.astype(BF)
    for n in range(D // NC):
        put(h, n, r0, silu_half(dot(x, w[:, cols(n)].astype(BF))).astype(BF))


def grid_weights(dst, tmp, w, bias):
    k = w.shape[0]
    tmp[0:LANES, :] = jnp.zeros((LANES, D), F32)
    tmp[0:k, :] = 0.5 * w[...].astype(F32)
    tmp[k:k + 1, :] = 0.5 * bias
    for j in range(NB):
        dst[j] = tmp[0:LANES, j * LANES:(j + 1) * LANES].astype(BF)


def grid_layer(x, w, h, r0):
    for n in range(D // NC):
        put(h, n, r0, silu_half(dot(x, rhs(w, n))).astype(BF))


def full_layer(a, w, h, r0, bias):
    for n in range(D // NC):
        pre = dot(a, rhs(w, n)) + bias[:, cols(n)]
        put(h, n, r0, silu_half(0.5 * pre).astype(BF))


def node_kernel(mf, xg, w_mesh, w_grid, vecs, wsec, wedge, wgrid, hm_out, proj_out, grid_out,
                xt, a1, a0, emb, h, r, b1, w3, b0, wg, b5, sems):
    copies = [column_copies(wsec.at[1], b1, sems.at[0]), column_copies(wedge.at[pl.ds(2 * D, D)], w3, sems.at[1]),
              column_copies(wsec.at[0], b0, sems.at[2]), column_copies(wgrid, wg, sems.at[3]),
              column_copies(wsec.at[5], b5, sems.at[4])]
    for c in copies:
        start(c)
    blocks = range(0, NODES, SUB)
    narrow_weights(a1, w_mesh, vec(vecs, 1, 0))
    grid_weights(a0, r, w_grid, vec(vecs, 0, 0))
    xt[...] = jnp.ones_like(xt)
    xt[0:mf.shape[0], :] = mf[...]
    for r0 in blocks:
        narrow_layer(xt, a1, h, r0)
    wait(copies[0])
    for r0 in blocks:
        second_layer(h, b1, r, r0, vec(vecs, 1, 1))
        norm_rows(r, r0, vecs, 1, lambda row, y: put_rows(hm_out, row, y.astype(BF)))
    wait(copies[1])
    for r0 in blocks:
        a = lhs(hm_out, r0)
        for n in range(D // NC):
            p = dot(a, rhs(w3, n)) + vec(vecs, 3, 0)[:, cols(n)]
            for t in range(2):
                proj_out[pl.ds(r0 * 8 + 2 * n + t, SUB, stride=8), :] = p[:, t * LANES:(t + 1) * LANES]
    for r0 in blocks:
        grid_layer(xg[r0:r0 + SUB, :], a0, h, r0)
    wait(copies[2])
    for r0 in blocks:
        second_layer(h, b0, r, r0, vec(vecs, 0, 1))
        norm_rows(r, r0, vecs, 0, lambda row, y: put_rows(emb, row, y.astype(BF)))
    wait(copies[3])
    for r0 in blocks:
        full_layer(lhs(emb, r0), wg, h, r0, vec(vecs, 5, 0))
    wait(copies[4])
    for r0 in blocks:
        second_layer(h, b5, r, r0, vec(vecs, 5, 1))

        def store(row, y):
            grid_out[row:row + LN_ROWS, :] = (get_rows(emb, row).astype(F32) + y).astype(BF)
        norm_rows(r, r0, vecs, 5, store)


def select_kernel(req, xg, out):
    xt = xg[...].T
    for k in range(EDGES // PICK):
        ids = req[:, k * PICK:(k + 1) * PICK]
        row = lax.broadcasted_iota(jnp.int32, (BAND, PICK), 0)
        hot = jnp.where(row == ids, 1.0, 0.0).astype(BF)
        out[k * PICK:(k + 1) * PICK, :] = dot(xt, hot).T.astype(BF)


def embed_kernel(ef, w_edge, vecs, wsec, he_out, xt, a2, h, r, b2, sems):
    c2 = column_copies(wsec.at[2], b2, sems.at[0])
    blocks = range(0, ROWS_E, SUB)

    @pl.when(pl.program_id(0) == 0)
    def _():
        start(c2)
        narrow_weights(a2, w_edge, vec(vecs, 2, 0))
        xt[...] = jnp.ones_like(xt)
        wait(c2)
    xt[0:ef.shape[0], :] = ef[...]
    narrow_layer(xt, a2, h, 0)
    for r0 in blocks:
        if r0 + SUB < ROWS_E:
            narrow_layer(xt, a2, h, r0 + SUB)
        second_layer(h, b2, r, r0, vec(vecs, 2, 1))
        norm_rows(r, r0, vecs, 2, lambda row, y: put_rows(he_out, row, y.astype(BF)))


def edge_kernel(src_s, dst_s, he, dst_v, mask_v, dst_p, mask_p, w_grid, vecs, hm, proj, table, wsec, wedge, wmesh, mesh_out,
                ftab, xg, gm, a0, h, r, ry, hg, newx, newy, hey, acc, b0, b3, w12, wm, b4, sems):
    i = pl.program_id(0)
    steps = EDGES // ROWS
    c0 = column_copies(wsec.at[0], b0, sems.at[0])
    c1 = column_copies(wedge.at[pl.ds(0, 2 * D)], w12, sems.at[1])
    c3 = column_copies(wsec.at[3], b3, sems.at[2])
    cm = column_copies(wmesh, wm, sems.at[3])
    c4 = column_copies(wsec.at[4], b4, sems.at[4])

    def fetch_row(edge, row):
        xg[pl.ds(row, 1), :] = ftab[pl.ds(src_s[edge], 1), :]

    @pl.when(i == 0)
    def _():
        for c in (c0, c1, c3, cm, c4):
            start(c)
        grid_weights(a0, r, w_grid, vec(vecs, 0, 0))
        acc[...] = jnp.zeros_like(acc)
        ry[...] = jnp.zeros_like(ry)
        hey[...] = jnp.zeros_like(hey)

        def widen(k, carry):
            rows = pl.ds(pl.multiple_of(k * 256, 256), 256)
            ftab[rows, :] = table[rows, :].astype(F32)
            return carry
        lax.fori_loop(0, EDGES // 256, widen, 0)

        def fetch8(k, carry):
            for t in range(8):
                fetch_row(k * 8 + t, k * 8 + t)
            return carry
        lax.fori_loop(0, ROWS // 8, fetch8, 0)
        for c in (c0, c1, c3):
            wait(c)

    def aggregate(dst, mask, new):
        node = lax.broadcasted_iota(jnp.int32, (NODES, SUB), 0)
        inc = jnp.where(node == jnp.where(mask > 0, dst, -1), 1.0, 0.0).astype(BF)
        for n in range(D // NC):
            acc[:, cols(n)] += dot(inc, rhs(new, n))

    def store_y(row, y):
        put_rows(newy, row, (get_rows(hey, row).astype(F32) + y).astype(BF))

    blocks = range(0, ROWS, SUB)
    for r0 in blocks:
        grid_layer(xg[r0:r0 + SUB, :].astype(BF), a0, h, r0)
    base = i * ROWS
    after = jnp.minimum(i + 1, steps - 1) * ROWS
    for e in range(ROWS):
        d = dst_s[base + e]
        gm[e * 8:(e + 1) * 8, :] = proj[pl.ds(pl.multiple_of(d * 8, 8), 8), :]
        fetch_row(after + e, e)
    norm_rows(ry, 0, vecs, 3, store_y)
    for r0 in blocks:
        second_layer(h, b0, r, r0, vec(vecs, 0, 1))
        norm_rows(r, r0, vecs, 0, lambda row, y: put_rows(hg, row, y.astype(BF)))
    for r0 in blocks:
        a = wide(lhs(he, r0), lhs(hg, r0))
        for n in range(D // NC):
            x = dot(a, rhs(w12, n))
            x = x + wide(*[gm[pl.ds(r0 * 8 + 2 * n + t, SUB, stride=8), :] for t in range(2)])
            put(h, n, r0, silu_half(0.5 * x).astype(BF))
    second_layer(h, b3, r, 0, vec(vecs, 3, 1))

    def store_x(row, y):
        put_rows(newx, row, (get_rows(he, row).astype(F32) + y).astype(BF))
    norm_rows(r, 0, vecs, 3, store_x)
    aggregate(dst_p[0, :, SUB:], mask_p[0, :, SUB:] * jnp.minimum(i, 1), newy)
    a = lhs(h, SUB)
    for n in range(D // NC):
        ry[:, cols(n)] = dot(a, rhs(b3, n)) + vec(vecs, 3, 1)[:, cols(n)]
    for j in range(NB):
        hey[j] = he[j, SUB:, :]
    aggregate(dst_v[0, :, :SUB], mask_v[0, :, :SUB], newx)

    @pl.when(i == steps - 1)
    def _():
        norm_rows(ry, 0, vecs, 3, store_y)
        wait(cm)
        wait(c4)
        aggregate(dst_v[0, :, SUB:], mask_v[0, :, SUB:], newy)
        for j in range(NB):
            hg[j] = acc[:, j * LANES:(j + 1) * LANES].astype(BF)
        for r0 in range(0, NODES, SUB):
            full_layer(wide(lhs(hm, r0), lhs(hg, r0)), wm, h, r0, vec(vecs, 4, 0))
        for r0 in range(0, NODES, SUB):
            second_layer(h, b4, r, r0, vec(vecs, 4, 1))

            def store(row, y):
                mesh_out[row:row + LN_ROWS, :] = (get_rows(hm, row).astype(F32) + y).astype(BF)
            norm_rows(r, r0, vecs, 4, store)


def fixed(shape):
    return pl.BlockSpec(shape, lambda i, *_: (0,) * len(shape), pipeline_mode=pl.Buffered(1))


FAR = pl.BlockSpec(memory_space=pltpu.HBM)
SQUARE = pltpu.VMEM((NB, D, LANES), BF)
HIDDEN = pltpu.VMEM((NB, ROWS, LANES), BF)
HALF = pltpu.VMEM((NB, SUB, LANES), BF)
RESULT = pltpu.VMEM((ROWS, D), F32)
VECS = (6, 4, D)
PARAMS = pltpu.CompilerParams(vmem_limit_bytes=67043328, dimension_semantics=("arbitrary",))


def cost(macs, size):
    return pl.CostEstimate(flops=2 * macs, bytes_accessed=size, transcendentals=0)


def run_nodes(mesh_t, xg, w_mesh_emb, w_grid_emb, vecs, w_second, w_edge_upd, w_grid_upd):
    return pl.pallas_call(
        node_kernel,
        grid=(1,),
        in_specs=[fixed(mesh_t.shape), fixed((BAND, LANES)), fixed(w_mesh_emb.shape), fixed(w_grid_emb.shape), fixed(VECS),
                  FAR, FAR, FAR],
        out_specs=[fixed((NB, NODES, LANES)), fixed((NODES * 8, LANES)), fixed((BAND, D))],
        out_shape=[jax.ShapeDtypeStruct((NB, NODES, LANES), BF), jax.ShapeDtypeStruct((NODES * 8, LANES), F32),
                   jax.ShapeDtypeStruct((BAND, D), BF)],
        scratch_shapes=[pltpu.VMEM((8, NODES), F32), pltpu.VMEM((8, D), F32), pltpu.VMEM((NB, LANES, LANES), BF), HIDDEN,
                        HIDDEN, RESULT, SQUARE, SQUARE, SQUARE, SQUARE, SQUARE, pltpu.SemaphoreType.DMA((5,))],
        compiler_params=PARAMS,
        cost_estimate=cost(NODES * D * (5 * D + 512), 16 << 20),
        name="nodes",
    )(mesh_t, xg, w_mesh_emb, w_grid_emb, vecs, w_second, w_edge_upd, w_grid_upd)


def run_select(req, xg):
    return pl.pallas_call(
        select_kernel,
        grid=(1,),
        in_specs=[fixed((1, EDGES)), fixed((BAND, LANES))],
        out_specs=fixed((EDGES, LANES)),
        out_shape=jax.ShapeDtypeStruct((EDGES, LANES), BF),
        compiler_params=PARAMS,
        cost_estimate=cost(EDGES * BAND * LANES, 3 << 20),
        name="select",
    )(req, xg)


def run_embed(edge_t, w_edge_emb, vecs, w_second):
    return pl.pallas_call(
        embed_kernel,
        grid=(EDGES // ROWS_E,),
        in_specs=[pl.BlockSpec((edge_t.shape[0], ROWS_E), lambda i: (0, i)), fixed(w_edge_emb.shape), fixed(VECS), FAR],
        out_specs=pl.BlockSpec((NB, ROWS_E, LANES), lambda i: (0, i, 0)),
        out_shape=jax.ShapeDtypeStruct((NB, EDGES, LANES), BF),
        scratch_shapes=[pltpu.VMEM((8, ROWS_E), F32), pltpu.VMEM((8, D), F32), pltpu.VMEM((NB, ROWS_E, LANES), BF),
                        pltpu.VMEM((ROWS_E, D), F32), SQUARE, pltpu.SemaphoreType.DMA((1,))],
        compiler_params=PARAMS,
        cost_estimate=cost(EDGES * D * (D + 256), 18 << 20),
        name="embed",
    )(edge_t, w_edge_emb, vecs, w_second)


def run_edges(src, dst, he, mask, w_grid_emb, vecs, hm, proj, table, w_second, w_edge_upd, w_mesh_upd):
    steps = EDGES // ROWS
    here = pl.BlockSpec((1, 1, ROWS), lambda i, *_: (i, 0, 0))
    before = pl.BlockSpec((1, 1, ROWS), lambda i, *_: (jnp.maximum(i - 1, 0), 0, 0))
    grid_spec = pltpu.PrefetchScalarGridSpec(
        num_scalar_prefetch=2,
        grid=(steps,),
        in_specs=[pl.BlockSpec((NB, ROWS, LANES), lambda i, *_: (0, i, 0)), here, here, before, before,
                  fixed(w_grid_emb.shape), fixed(VECS), fixed((NB, NODES, LANES)), fixed((NODES * 8, LANES)),
                  fixed((EDGES, LANES)), FAR, FAR, FAR],
        out_specs=fixed((NODES, D)),
        scratch_shapes=[pltpu.VMEM((EDGES, LANES), F32), pltpu.VMEM((ROWS, LANES), F32), pltpu.VMEM((ROWS * 8, LANES), F32),
                        pltpu.VMEM((NB, LANES, LANES), BF), HIDDEN, RESULT, pltpu.VMEM((SUB, D), F32), HIDDEN,
                        HALF, HALF, HALF, pltpu.VMEM((NODES, D), F32),
                        SQUARE, SQUARE, pltpu.VMEM((NB, 2 * D, LANES), BF), pltpu.VMEM((NB, 2 * D, LANES), BF), SQUARE,
                        pltpu.SemaphoreType.DMA((5,))])
    dst3 = dst.reshape(steps, 1, ROWS)
    mask3 = mask.reshape(steps, 1, ROWS)
    return pl.pallas_call(
        edge_kernel,
        grid_spec=grid_spec,
        out_shape=jax.ShapeDtypeStruct((NODES, D), BF),
        compiler_params=PARAMS,
        cost_estimate=cost(EDGES * D * (4 * D + 256 + NODES) + NODES * 3 * D * D, 40 << 20),
        name="edges",
    )(src, dst, he, dst3, mask3, dst3, mask3, w_grid_emb, vecs, hm, proj, table, w_second, w_edge_upd, w_mesh_upd)


def pad_features(x):
    ones = jnp.ones((x.shape[0], 1), BF)
    return jnp.concatenate([x.astype(BF), ones, jnp.zeros((x.shape[0], LANES - 1 - x.shape[1]), BF)], axis=1)


def exchange(x):
    return lax.all_to_all(x, 'graph', 0, 0, tiled=True)


def solution(mesh):
    size = mesh.shape['graph']
    sharded = P(('batch', 'graph'))
    replicated = P()

    def local_step(grid_feat, mesh_feat, edge_feat, need_rows, edge_src, edge_dst, edge_mask,
                   w_grid_emb, w_mesh_emb, w_edge_emb, w_edge_upd, w_mesh_upd, w_grid_upd, w_second, mlp_vecs):
        slots = need_rows.shape[0] // size
        wanted = exchange(need_rows.reshape(size, slots))
        xg = pad_features(grid_feat)
        vecs = mlp_vecs.astype(F32)
        hm, proj, grid_out = run_nodes(mesh_feat.T, xg, w_mesh_emb, w_grid_emb, vecs, w_second, w_edge_upd, w_grid_upd)
        wanted, hm = lax.optimization_barrier((wanted, hm))
        rows = run_select(wanted.reshape(1, size * slots), xg)
        rows, vecs = lax.optimization_barrier((rows, vecs))
        table = exchange(rows.reshape(size, slots, LANES)).reshape(size * slots, LANES)
        he = run_embed(edge_feat.T, w_edge_emb, vecs, w_second)
        mesh_out = run_edges(edge_src, edge_dst, he, edge_mask, w_grid_emb, vecs, hm, proj, table,
                             w_second, w_edge_upd, w_mesh_upd)
        return mesh_out, grid_out

    return jax.shard_map(local_step, mesh=mesh,
                         in_specs=(sharded,) * 7 + (replicated,) * 8,
                         out_specs=(sharded, sharded), check_vma=False)
```

time: 554 us -> 196 us (0.35)
  the two profiles are of different devices: /device:TPU:37 before, /device:TPU:1 now
where the time goes in v3:
time: 196 us
  Pallas kernels  166 us (85%)
  starting transfers between devices  22.2 us (11%)
  local copies, waits for them, and re-layouts  3.3 us (2%)
  other arithmetic  3.09 us (2%)
    pallas_call x1, Pallas kernels, run_edges(): pl.pallas_call(edge_kernel, grid_spec=grid_spec, out_shape=jax.ShapeDtype...  115 us
    pallas_call x1, Pallas kernels, run_embed(): pl.pallas_call(embed_kernel, grid=(EDGES // ROWS_E,), in_specs=[pl.BlockS...  34.2 us
    all_to_all x2, starting transfers between devices, exchange(): return lax.all_to_all(x, 'graph', 0, 0, tiled=True)  22.2 us
    pallas_call x1, Pallas kernels, run_nodes(): pl.pallas_call(node_kernel, grid=(1,), in_specs=[fixed(mesh_t.shape), fix...  11.7 us
    pallas_call x1, Pallas kernels, run_select(): pl.pallas_call(select_kernel, grid=(1,), in_specs=[fixed((1, EDGES)), fix...  5.12 us
  transfers between devices with their start and end apart: 2, of which 0 were waited for; matrix products, arithmetic and copies ran while one was open for 2% of the time, Pallas kernels for 23%

profile of v3, /device:TPU:1, one launch (start us, length us, event | category | flops | bytes accessed | tf_op | source)
XLA Modules:
  0.0 195.6 jit_solution(11585118888030024681)
XLA Ops:
  0.6 1.5 all_to_all.11
  2.1 12.0 %all-to-all-start = ((s32[128,1,64]{2,1,0:T(1,128)}), s32[128,1,64]{2,1,0:T(1,128)}, u32[]{:S(2)}, u32[]{:S(2)}) async-start(s32[128,1,64]{2,1,0:T(1,128)} %bitcast.1), calls=%async_computation | async-start | bytes 131072 | tf_op jit(solution)/shard_map/all_to_all | solution.py:394
  14.0 0.1 pad.1.clone
  14.1 0.1 pad.2.clone
  14.2 1.4 convert_element_type.7.vecs
  15.7 0.9 convert_element_type.6
  16.6 0.1 copy.22
  16.7 0.7 maximum_maximum_fusion.xg
  17.4 11.7 %nodes.1 = (bf16[8,512,128]{2,1,0:T(8,128)(2,1)}, f32[4096,128]{1,0:T(8,128)}, bf16[512,1024]{1,0:T(8,128)(2,1)}) custom-call(f32[3,512]{1,0:T(4,128)} %bitcast.15, bf16[512,128]{1,0:T(8,128)(2,1)} %maximum_maximum_fusion.xg, bf16[3,1024]{1,0:T(4,128)(2,1)} %w_mesh.1, bf16[102,1024]{1,0:T(8,128)(2,1)} %w_grid.3, f32[6,4,1024]{2,1,0:T(4,128)} %convert_element_type.7.vecs, ...), custom_call_target="tpu_custom_call" | custom-call | flops 5905580032 | bytes 16777216 | tf_op jit(solution)/shard_map/nodes/pallas_call | solution.py:316
  29.1 0.0 all-to-all-done
  29.1 1.6 reshape.23.req
  30.7 5.1 %select.1 = bf16[8192,128]{1,0:T(8,128)(2,1)} custom-call(s32[1,8192]{1,0:T(1,128)} %reshape.23.req, bf16[512,128]{1,0:T(8,128)(2,1)} %maximum_maximum_fusion.xg), custom_call_target="tpu_custom_call" | custom-call | flops 1073741824 | bytes 3145728 | tf_op jit(solution)/shard_map/select/pallas_call | solution.py:333
  35.8 10.2 %all-to-all-start.1 = ((bf16[128,64,128]{2,1,0:T(8,128)(2,1)}), bf16[128,64,128]{2,1,0:T(8,128)(2,1)}, u32[]{:S(2)}, u32[]{:S(2)}) async-start(bf16[128,64,128]{2,1,0:T(8,128)(2,1)} %bitcast.9), calls=%async_computation.1 | async-start | bytes 4194304 | tf_op jit(solution)/shard_map/all_to_all | solution.py:394
  46.1 34.2 %embed.1.he = bf16[8,8192,128]{2,1,0:T(8,128)(2,1)} custom-call(f32[4,8192]{1,0:T(4,128)} %bitcast.10, bf16[4,1024]{1,0:T(4,128)(2,1)} %w_edge.1, f32[6,4,1024]{2,1,0:T(4,128)} %convert_element_type.7.vecs, bf16[6,1024,1024]{2,1,0:T(8,128)(2,1)} %wsec.5), custom_call_target="tpu_custom_call" | custom-call | flops 21474836480 | bytes 18874368 | tf_op jit(solution)/shard_map/embed/pallas_call | solution.py:346
  80.3 0.0 all-to-all-done.1
  80.3 115.1 %edges.1 = bf16[512,1024]{1,0:T(8,128)(2,1)} custom-call(s32[8192]{0:T(1024)} %src_s.1, s32[8192]{0:T(1024)} %dst_s.1, bf16[8,8192,128]{2,1,0:T(8,128)(2,1)} %embed.1.he, s32[16,1,512]{2,1,0:T(1,128)} %bitcast.11, s32[16,1,512]{2,1,0:T(1,128)} %bitcast.13, s32[16,1,512]{2,1,0:T(1,128)} %bitcast.12, s32[16,1,512]{2,1,0:T(1,128)} %bitcast.14, ...), custom_call_target="tpu_custom_call" | custom-call | flops 84825604096 | bytes 41943040 | tf_op jit(solution)/shard_map/edges/pallas_call | solution.py:378
  (1 shorter events, 0.0 us)
Async XLA Ops:
  2.1 27.1 %all-to-all-start = ((s32[128,1,64]{2,1,0:T(1,128)}), s32[128,1,64]{2,1,0:T(1,128)}, u32[]{:S(2)}, u32[]{:S(2)}) async-start(s32[128,1,64]{2,1,0:T(1,128)} %bitcast.1), calls=%async_computation | async-start | bytes 131072 | tf_op jit(solution)/shard_map/all_to_all | solution.py:394
  35.8 44.5 %all-to-all-start.1 = ((bf16[128,64,128]{2,1,0:T(8,128)(2,1)}), bf16[128,64,128]{2,1,0:T(8,128)(2,1)}, u32[]{:S(2)}, u32[]{:S(2)}) async-start(bf16[128,64,128]{2,1,0:T(8,128)(2,1)} %bitcast.9), calls=%async_computation.1 | async-start | bytes 4194304 | tf_op jit(solution)/shard_map/all_to_all | solution.py:394
